TPU v7x, 32 devices: a whole 2x2x4 slice. The times are simulated.
32 devices in a mesh: dp: 4 (over y, core), mp: 2 (over x), section: 4 (over z).
Axes of the slice: x: 2, y: 2, z: 4, core: 2. Of those that a mesh axis runs over, the one named last changes fastest.
Arguments:
- hidden_in: bfloat16 [64, 2560], P('dp', 'mp'), may hold values from -6 to 6
- lengths: int32 [64], P('dp'), may hold values from 0 to 7
- slots: int32 [64], P('dp'), may hold values from 0 to 71, as said below
- norm_gain: float32 [4, 2560], P('section'), may hold values from 0.5 to 1.5
- w_zxo: bfloat16 [4, 3, 5120, 2560], P('section', None, 'dp', 'mp'), may hold values from -0.125 to 0.125
- w_bcdt: bfloat16 [4, 336, 2560], P('section', 'dp', 'mp'), may hold values from -0.125 to 0.125
- conv_x_weight: float32 [4, 4, 5120], P('section', None, 'mp'), may hold values from -0.5 to 0.5
- conv_bc_weight: float32 [4, 4, 256], P('section'), may hold values from -0.5 to 0.5
- conv_x_pool: bfloat16 [4, 72, 3, 5120], P('section', 'dp', None, 'mp'), may hold values from -6 to 6
- conv_bc_pool: bfloat16 [4, 72, 3, 256], P('section', 'dp'), may hold values from -6 to 6
- state_pool: float32 [4, 72, 80, 64, 128], P('section', 'dp', 'mp'), may hold values from -1 to 1
- a_rate: float32 [4, 80], P('section', 'mp'), may hold values from 1 to 16
- dt_bias: float32 [4, 80], P('section', 'mp'), may hold values from -3 to 0
- skip_gain: float32 [4, 80], P('section', 'mp'), may hold values from 0.5 to 1.5
- gate_gain: float32 [4, 5120], P('section', 'mp'), may hold values from 0.5 to 1.5
Outputs:
- hidden_out: bfloat16 [4, 64, 2560], P('section', 'dp', 'mp')
- state_out: float32 [4, 64, 80, 64, 128], P('section', 'dp', 'mp')
Inputs may be any that keep to these rules, and one draw needn't show every extreme that they name: The sequences of the d-th block of 16 name distinct slots, all from d * 18 to (d + 1) * 18 - 1.
All inputs are finite; a program needn't handle non-finite values.
Results may differ from a plain program's by a relative error of at most 0.025.
Values may be sent and summed in bfloat16 or wider, within the bound.
No kernel may reach another device: no remote copies, remote signals or barrier semaphores. Data moves between devices by JAX's collectives and lax.ppermute only.
A program may use at most 192 MiB of HBM per device.

v0:
```python
import jax
import jax.numpy as jnp
from jax import lax
from jax.sharding import PartitionSpec as P

MICRO = 4


epsilon = 1e-05


def passed_along(array, axis, by):
    devices = lax.axis_size(axis)
    pairs = [(i, i + by) for i in range(devices) if 0 <= i + by < devices]
    return lax.ppermute(array, axis, pairs)


def project(inputs, weights):
    return lax.dot_general(
        inputs, weights, (((1,), (1,)), ((), ())), preferred_element_type=jnp.float32
    )


def convolve(history, current, kernel, tap_mask):
    past_sum = jnp.sum(
        history.astype(jnp.float32) * tap_mask[:, :, None] * kernel[None, :3, :], axis=1
    )
    return jax.nn.silu(past_sum + current * kernel[3][None, :])


def local(
    hidden_in,
    lengths,
    slots,
    norm_gain,
    w_zxo,
    w_bcdt,
    conv_x_weight,
    conv_bc_weight,
    conv_x_pool,
    conv_bc_pool,
    state_pool,
    a_rate,
    dt_bias,
    skip_gain,
    gate_gain,
):
    section_index = lax.axis_index("section")
    section_count = lax.axis_size("section")
    mp_index = lax.axis_index("mp")
    mp_count = lax.axis_size("mp")
    dp_index = lax.axis_index("dp")
    dp_count = lax.axis_size("dp")
    seq_dev = hidden_in.shape[0]
    micro_rows = seq_dev // MICRO
    model_width = norm_gain.shape[1]
    model_share = hidden_in.shape[1]
    heads_dev = a_rate.shape[1]
    head_size = state_pool.shape[3]
    state_size = state_pool.shape[4]
    chan_dev = heads_dev * head_size
    slots_dev = state_pool.shape[1]
    bc_width = conv_bc_weight.shape[2]
    half_width = bc_width // 2
    chan_saved = w_zxo.shape[2]
    chan_total = chan_saved * dp_count
    chan_group = chan_total // mp_count
    piece_rows = min(chan_saved, chan_group)
    row_count = max(1, chan_group // chan_saved)
    first_row = mp_index * chan_group // chan_saved
    piece_offset = jnp.clip(
        mp_index * chan_group - dp_index * chan_saved, 0, chan_saved - piece_rows
    )
    entry_full = lax.all_gather(hidden_in, "mp", axis=1, tiled=True)
    pre_gain = norm_gain[0]
    post_gain = gate_gain[0]
    kernel_x = conv_x_weight[0]
    kernel_bc = conv_bc_weight[0]
    rate_heads = a_rate[0]
    bias_heads = dt_bias[0]
    skip_heads = skip_gain[0]
    local_slots = slots - dp_index * slots_dev
    tick_count = MICRO + section_count - 1
    hidden_buffer = jnp.zeros((seq_dev, model_share), jnp.bfloat16)
    state_buffer = jnp.zeros((seq_dev, heads_dev, head_size, state_size), jnp.float32)
    received = None
    for tick_index in range(tick_count):
        if tick_index < MICRO:
            first_rows = entry_full[tick_index * micro_rows : (tick_index + 1) * micro_rows]
        else:
            first_rows = jnp.zeros((micro_rows, model_width), jnp.bfloat16)
        if tick_index == 0:
            layer_input = first_rows
        else:
            layer_input = jnp.where(section_index == 0, first_rows, received)
        micro_index = tick_index - section_index
        in_range = (micro_index >= 0) & (micro_index < MICRO)
        row_start = jnp.clip(micro_index, 0, MICRO - 1) * micro_rows
        rows_length = lax.dynamic_slice_in_dim(lengths, row_start, micro_rows)
        rows_slot = lax.dynamic_slice_in_dim(local_slots, row_start, micro_rows)
        tap_mask = (rows_length[:, None] >= (3 - jnp.arange(3, dtype=jnp.int32))[None, :]).astype(
            jnp.float32
        )
        alive = (rows_length > 0).astype(jnp.float32)
        residual = layer_input.astype(jnp.float32)
        normed_in = (
            residual
            * lax.rsqrt(jnp.mean(residual * residual, axis=1, keepdims=True) + epsilon)
            * pre_gain[None, :]
        ).astype(jnp.bfloat16)
        normed_share = lax.dynamic_slice_in_dim(normed_in, mp_index * model_share, model_share, 1)
        rows_all = lax.all_gather(normed_share, "dp", axis=0, tiled=True)
        zx_part = jnp.einsum(
            "rf,kcf->rkc", rows_all, w_zxo[0, :2], preferred_element_type=jnp.float32
        )
        small_part = project(rows_all, w_bcdt[0])
        zx_sum, small_sum = (
            lax.psum(zx_part.astype(jnp.bfloat16), "mp").astype(jnp.float32),
            lax.psum(small_part.astype(jnp.bfloat16), "mp").astype(jnp.float32),
        )
        zx_send = lax.dynamic_slice_in_dim(zx_sum, piece_offset, piece_rows, 2)
        zx_got, small_got = (
            lax.all_to_all(
                zx_send.astype(jnp.bfloat16), "dp", split_axis=0, concat_axis=0, tiled=True
            ).astype(zx_send.dtype),
            lax.all_to_all(
                small_sum.astype(jnp.bfloat16), "dp", split_axis=0, concat_axis=0, tiled=True
            ).astype(small_sum.dtype),
        )
        zx_blocks = zx_got.reshape(dp_count, micro_rows, 2, piece_rows)
        zx_picked = lax.dynamic_slice_in_dim(zx_blocks, first_row, row_count, 0)
        zx_mine = jnp.transpose(zx_picked, (1, 2, 0, 3)).reshape(micro_rows, 2, chan_dev)
        gate_proj = zx_mine[:, 0]
        inner_proj = zx_mine[:, 1]
        small_proj = jnp.transpose(
            small_got.reshape(dp_count, micro_rows, small_got.shape[1]), (1, 0, 2)
        ).reshape(micro_rows, dp_count * small_got.shape[1])
        step_raw = lax.dynamic_slice_in_dim(
            small_proj, bc_width + mp_index * heads_dev, heads_dev, 1
        )
        conv_x = convolve(
            jnp.take(conv_x_pool[0], rows_slot, axis=0), inner_proj, kernel_x, tap_mask
        )
        conv_bc = convolve(
            jnp.take(conv_bc_pool[0], rows_slot, axis=0),
            small_proj[:, :bc_width],
            kernel_bc,
            tap_mask,
        )
        conv_b = conv_bc[:, :half_width]
        conv_c = conv_bc[:, half_width:]
        step_size = jax.nn.softplus(step_raw + bias_heads[None, :])
        decay_rate = jnp.exp(-step_size * rate_heads[None, :])
        old_state = jnp.take(state_pool[0], rows_slot, axis=0) * alive[:, None, None, None]
        inner_heads = conv_x.reshape(micro_rows, heads_dev, head_size)
        new_state = (
            decay_rate[:, :, None, None] * old_state
            + (step_size[:, :, None] * inner_heads)[:, :, :, None] * conv_b[:, None, None, :]
        )
        read_out = (
            jnp.einsum("bhpn,bn->bhp", new_state, conv_c, precision=lax.Precision.HIGHEST)
            + skip_heads[None, :, None] * inner_heads
        )
        gated = read_out.reshape(micro_rows, chan_dev) * jax.nn.silu(gate_proj)
        square_sum = lax.psum(jnp.sum(gated * gated, axis=1), "mp")
        normed = (
            gated
            * lax.rsqrt(square_sum[:, None] / (chan_dev * mp_count) + epsilon)
            * post_gain[None, :]
        ).astype(jnp.bfloat16)
        all_channels = lax.all_gather(normed, "mp", axis=1, tiled=True)
        block_rows = lax.all_to_all(all_channels, "dp", split_axis=1, concat_axis=0, tiled=True)
        partial_rows = jnp.dot(block_rows, w_zxo[0, 2], preferred_element_type=jnp.float32)
        summed = lax.psum_scatter(partial_rows, "dp", scatter_dimension=0, tiled=True)
        residual_share = lax.dynamic_slice_in_dim(residual, mp_index * model_share, model_share, 1)
        new_share = (residual_share + summed).astype(jnp.bfloat16)
        outgoing = lax.all_gather(new_share, "mp", axis=1, tiled=True)
        current_hidden = lax.dynamic_slice_in_dim(hidden_buffer, row_start, micro_rows, 0)
        hidden_buffer = lax.dynamic_update_slice_in_dim(
            hidden_buffer, jnp.where(in_range, new_share, current_hidden), row_start, 0
        )
        current_state = lax.dynamic_slice_in_dim(state_buffer, row_start, micro_rows, 0)
        state_buffer = lax.dynamic_update_slice_in_dim(
            state_buffer, jnp.where(in_range, new_state, current_state), row_start, 0
        )
        if tick_index + 1 < tick_count:
            received = passed_along(outgoing, "section", 1)
    return (hidden_buffer[None], state_buffer[None])


def solution(mesh):
    placed = (
        P("dp", "mp"),
        P("dp"),
        P("dp"),
        P("section", None),
        P("section", None, "dp", "mp"),
        P("section", "dp", "mp"),
        P("section", None, "mp"),
        P("section", None, None),
        P("section", "dp", None, "mp"),
        P("section", "dp", None, None),
        P("section", "dp", "mp", None, None),
        P("section", "mp"),
        P("section", "mp"),
        P("section", "mp"),
        P("section", "mp"),
    )
    return jax.shard_map(
        local,
        mesh=mesh,
        in_specs=placed,
        out_specs=(P("section", "dp", "mp"), P("section", "dp", "mp", None, None)),
        check_vma=False,
    )
```

profile of v0, /device:TPU:0, one launch (start us, length us, event | category | flops | bytes accessed | tf_op | source)
XLA Modules:
  0.0 981.9 jit_solution(18190037035789719761)
XLA Ops:
  7.3 6.0 all_gather.63
  14.4 5.2 all-gather
  19.6 5.3 fusion.98
  25.1 5.5 psum.147
  36.1 11.0 %gather_fusion = f32[4,40,64,128]{3,2,1,0:T(8,128)} fusion(f32[18,40,64,128]{3,2,1,0:T(8,128)} %bitcast.323, s32[1024]{0:T(1024)S(1)} %pad_clamp_fusion.6), kind=kCustom, calls=%fused_computation.clone | custom fusion | bytes 10485776 | tf_op jit(solution)/shard_map/jit(_take)/gather | solution.py:154
  57.6 14.5 %fusion.28 = f32[4,1,40,64]{3,1,2,0:T(1,128)S(1)} fusion(f32[4,128,1,1]{1,2,3,0:T(1,128)S(1)} %bitcast.412, f32[4,40,64,128]{3,2,1,0:T(8,128)} %gather_fusion, f32[4,128]{1,0:T(4,128)S(1)} %get-tuple-element.118, f32[4,40,64]{2,1,0:T(8,128)S(1)} %broadcast_multiply_fusion.6, f32[4]{0:T(128)S(1)} %get-tuple-element.153, f32[4,40]{1,0:T(4,128)S(1)} %get-tuple-element.87, ...), kind=kOutput, calls=%fused_computation.63 | convolution fusion | flops 22282240 | bytes 5329556 | tf_op jit(solution)/shard_map/bhpn,bn->bhp/dot_general | solution.py:161
  72.4 4.9 psum.149
  98.0 26.3 %all-reduce.36.cloned.1.call-done = f32[16,1280]{1,0:T(8,128)} async-done(((f32[16,1280]{1,0:T(8,128)}), f32[16,1280]{1,0:T(8,128)}) %all-reduce.36.cloned.1.call-update) | async-done | bytes 81936
  133.1 10.9 %gather_fusion.3 = f32[4,40,64,128]{3,2,1,0:T(8,128)} fusion(f32[18,40,64,128]{3,2,1,0:T(8,128)} %bitcast.324, s32[1024]{0:T(1024)S(1)} %pad_clamp_fusion.5), kind=kCustom, calls=%fused_computation.3.clone | custom fusion | bytes 10485776 | tf_op jit(solution)/shard_map/jit(_take)/gather | solution.py:154
  144.3 5.2 all-gather.1
  149.7 5.5 psum.150
  158.8 5.3 fusion.101
  164.2 21.5 %all-reduce.24.cloned.1.call-done = bf16[16,2,1280]{2,0,1:T(8,128)(2,1)} async-done(((bf16[16,2,1280]{2,0,1:T(8,128)(2,1)}), bf16[16,2,1280]{2,0,1:T(8,128)(2,1)}) %all-reduce.24.cloned.1.call-update) | async-done | bytes 81936 | tf_op jit(solution)/shard_map/psum | solution.py:118
  195.4 14.5 %fusion.30 = f32[4,1,40,64]{3,1,2,0:T(1,128)S(1)} fusion(f32[4,128,1,1]{1,2,3,0:T(1,128)S(1)} %bitcast.407, f32[4,40,64,128]{3,2,1,0:T(8,128)} %gather_fusion.3, f32[4,128]{1,0:T(4,128)S(1)} %get-tuple-element.116, f32[4,40,64]{2,1,0:T(8,128)S(1)} %broadcast_multiply_fusion.5, f32[4]{0:T(128)S(1)} %get-tuple-element.155, ...), kind=kOutput, calls=%fused_computation.64 | convolution fusion | flops 22282240 | bytes 5329556 | tf_op jit(solution)/shard_map/bhpn,bn->bhp/dot_general | solution.py:161
  219.7 6.3 all_to_all.231
  229.2 29.5 %all-reduce.38.cloned.1.call-done = f32[16,1280]{1,0:T(8,128)} async-done(((f32[16,1280]{1,0:T(8,128)}), f32[16,1280]{1,0:T(8,128)}) %all-reduce.38.cloned.1.call-update) | async-done | bytes 81936
  267.3 11.0 %gather_fusion.6 = f32[4,40,64,128]{3,2,1,0:T(8,128)} fusion(f32[18,40,64,128]{3,2,1,0:T(8,128)} %bitcast.325, s32[1024]{0:T(1024)S(1)} %pad_clamp_fusion.4), kind=kCustom, calls=%fused_computation.4.clone | custom fusion | bytes 10485776 | tf_op jit(solution)/shard_map/jit(_take)/gather | solution.py:154
  278.6 5.2 all-gather.2
  284.0 5.5 psum.153
  292.8 5.3 fusion.104
  298.3 21.5 %all-reduce.26.cloned.1.call-done = bf16[16,2,1280]{2,0,1:T(8,128)(2,1)} async-done(((bf16[16,2,1280]{2,0,1:T(8,128)(2,1)}), bf16[16,2,1280]{2,0,1:T(8,128)(2,1)}) %all-reduce.26.cloned.1.call-update) | async-done | bytes 81936 | tf_op jit(solution)/shard_map/psum | solution.py:118
  329.5 14.5 %fusion.32 = f32[4,1,40,64]{3,1,2,0:T(1,128)S(1)} fusion(f32[4,128,1,1]{1,2,3,0:T(1,128)S(1)} %bitcast.408, f32[4,40,64,128]{3,2,1,0:T(8,128)} %gather_fusion.6, f32[4,128]{1,0:T(4,128)S(1)} %get-tuple-element.114, f32[4,40,64]{2,1,0:T(8,128)S(1)} %broadcast_multiply_fusion.4, f32[4]{0:T(128)S(1)} %get-tuple-element.157, ...), kind=kOutput, calls=%fused_computation.65 | convolution fusion | flops 22282240 | bytes 5329556 | tf_op jit(solution)/shard_map/bhpn,bn->bhp/dot_general | solution.py:161
  344.3 4.9 psum.155
  353.8 6.3 all_to_all.232
  363.2 29.5 %all-reduce.40.cloned.1.call-done = f32[16,1280]{1,0:T(8,128)} async-done(((f32[16,1280]{1,0:T(8,128)}), f32[16,1280]{1,0:T(8,128)}) %all-reduce.40.cloned.1.call-update) | async-done | bytes 81936
  401.3 10.9 %gather_fusion.9 = f32[4,40,64,128]{3,2,1,0:T(8,128)} fusion(f32[18,40,64,128]{3,2,1,0:T(8,128)} %bitcast.326, s32[1024]{0:T(1024)S(1)} %pad_clamp_fusion.3), kind=kCustom, calls=%fused_computation.5.clone | custom fusion | bytes 10485776 | tf_op jit(solution)/shard_map/jit(_take)/gather | solution.py:154
  412.5 5.2 all-gather.3
  417.9 5.5 psum.156
  426.7 5.3 fusion.107
  432.2 21.5 %all-reduce.28.cloned.1.call-done = bf16[16,2,1280]{2,0,1:T(8,128)(2,1)} async-done(((bf16[16,2,1280]{2,0,1:T(8,128)(2,1)}), bf16[16,2,1280]{2,0,1:T(8,128)(2,1)}) %all-reduce.28.cloned.1.call-update) | async-done | bytes 81936 | tf_op jit(solution)/shard_map/psum | solution.py:118
  463.4 14.5 %fusion.34 = f32[4,1,40,64]{3,1,2,0:T(1,128)S(1)} fusion(f32[4,128,1,1]{1,2,3,0:T(1,128)S(1)} %bitcast.409, f32[4,40,64,128]{3,2,1,0:T(8,128)} %gather_fusion.9, f32[4,128]{1,0:T(4,128)S(1)} %get-tuple-element.112, f32[4,40,64]{2,1,0:T(8,128)S(1)} %broadcast_multiply_fusion.3, f32[4]{0:T(128)S(1)} %get-tuple-element.159, ...), kind=kOutput, calls=%fused_computation.66 | convolution fusion | flops 22282240 | bytes 5329556 | tf_op jit(solution)/shard_map/bhpn,bn->bhp/dot_general | solution.py:161
  478.2 5.1 psum.158
  487.9 6.3 all_to_all.233
  497.3 29.5 %all-reduce.42.cloned.1.call-done = f32[16,1280]{1,0:T(8,128)} async-done(((f32[16,1280]{1,0:T(8,128)}), f32[16,1280]{1,0:T(8,128)}) %all-reduce.42.cloned.1.call-update) | async-done | bytes 81936
  535.4 10.9 %gather_fusion.12 = f32[4,40,64,128]{3,2,1,0:T(8,128)} fusion(f32[18,40,64,128]{3,2,1,0:T(8,128)} %bitcast.327, s32[1024]{0:T(1024)S(1)} %pad_clamp_fusion.2), kind=kCustom, calls=%fused_computation.6.clone | custom fusion | bytes 10485776 | tf_op jit(solution)/shard_map/jit(_take)/gather | solution.py:154
  546.7 5.2 all-gather.4
  552.1 5.5 psum.159
  560.9 5.3 fusion.110
  566.4 21.5 %all-reduce.30.cloned.1.call-done = bf16[16,2,1280]{2,0,1:T(8,128)(2,1)} async-done(((bf16[16,2,1280]{2,0,1:T(8,128)(2,1)}), bf16[16,2,1280]{2,0,1:T(8,128)(2,1)}) %all-reduce.30.cloned.1.call-update) | async-done | bytes 81936 | tf_op jit(solution)/shard_map/psum | solution.py:118
  597.6 14.5 %fusion.36 = f32[4,1,40,64]{3,1,2,0:T(1,128)S(1)} fusion(f32[4,128,1,1]{1,2,3,0:T(1,128)S(1)} %bitcast.410, f32[4,40,64,128]{3,2,1,0:T(8,128)} %gather_fusion.12, f32[4,128]{1,0:T(4,128)S(1)} %get-tuple-element.110, f32[4,40,64]{2,1,0:T(8,128)S(1)} %broadcast_multiply_fusion.2, f32[4]{0:T(128)S(1)} %get-tuple-element.161, ...), kind=kOutput, calls=%fused_computation.67 | convolution fusion | flops 22282240 | bytes 5329556 | tf_op jit(solution)/shard_map/bhpn,bn->bhp/dot_general | solution.py:161
  625.3 10.8 %gather_fusion.15 = f32[4,40,64,128]{3,2,1,0:T(8,128)} fusion(f32[18,40,64,128]{3,2,1,0:T(8,128)} %bitcast.328, s32[1024]{0:T(1024)S(1)} %pad_clamp_fusion.1), kind=kCustom, calls=%fused_computation.7.clone | custom fusion | bytes 10485776 | tf_op jit(solution)/shard_map/jit(_take)/gather | solution.py:154
  636.2 10.8 %gather_fusion.18 = f32[4,40,64,128]{3,2,1,0:T(8,128)} fusion(f32[18,40,64,128]{3,2,1,0:T(8,128)} %bitcast.329, s32[1024]{0:T(1024)S(1)} %pad_clamp_fusion), kind=kCustom, calls=%fused_computation.8.clone | custom fusion | bytes 10485776 | tf_op jit(solution)/shard_map/jit(_take)/gather | solution.py:154
  650.5 9.7 broadcast_in_dim.42
  663.9 17.5 %all-reduce.44.cloned.1.call-done = f32[16,1280]{1,0:T(8,128)} async-done(((f32[16,1280]{1,0:T(8,128)}), f32[16,1280]{1,0:T(8,128)}) %all-reduce.44.cloned.1.call-update) | async-done | bytes 81936
  690.1 8.1 select_dynamic-update-slice_fusion.4
  698.4 5.2 all-gather.5
  703.8 5.5 psum.162
  712.7 5.3 fusion.113
  718.1 21.6 %all-reduce.32.cloned.1.call-done = bf16[16,2,1280]{2,0,1:T(8,128)(2,1)} async-done(((bf16[16,2,1280]{2,0,1:T(8,128)(2,1)}), bf16[16,2,1280]{2,0,1:T(8,128)(2,1)}) %all-reduce.32.cloned.1.call-update) | async-done | bytes 81936 | tf_op jit(solution)/shard_map/psum | solution.py:118
  749.4 14.5 %fusion.38 = f32[4,1,40,64]{3,1,2,0:T(1,128)S(1)} fusion(f32[4,128,1,1]{1,2,3,0:T(1,128)S(1)} %bitcast.411, f32[4,40,64,128]{3,2,1,0:T(8,128)} %gather_fusion.15, f32[4,128]{1,0:T(4,128)S(1)} %get-tuple-element.108, f32[4,40,64]{2,1,0:T(8,128)S(1)} %broadcast_multiply_fusion.1, f32[4]{0:T(128)S(1)} %get-tuple-element.163, ...), kind=kOutput, calls=%fused_computation.68 | convolution fusion | flops 22282240 | bytes 5329556 | tf_op jit(solution)/shard_map/bhpn,bn->bhp/dot_general | solution.py:161
  764.2 4.9 psum.164
  777.1 8.0 select_dynamic-update-slice_fusion.3
  788.3 8.1 select_dynamic-update-slice_fusion.2
  796.5 22.8 %all-reduce.46.cloned.1.call-done = f32[16,1280]{1,0:T(8,128)} async-done(((f32[16,1280]{1,0:T(8,128)}), f32[16,1280]{1,0:T(8,128)}) %all-reduce.46.cloned.1.call-update) | async-done | bytes 81936
  827.8 8.1 select_dynamic-update-slice_fusion.1
  836.2 5.2 all-gather.6
  841.6 5.5 psum.165
  850.4 5.3 fusion.116
  855.9 21.4 %all-reduce.34.cloned.1.call-done = bf16[16,2,1280]{2,0,1:T(8,128)(2,1)} async-done(((bf16[16,2,1280]{2,0,1:T(8,128)(2,1)}), bf16[16,2,1280]{2,0,1:T(8,128)(2,1)}) %all-reduce.34.cloned.1.call-update) | async-done | bytes 81936 | tf_op jit(solution)/shard_map/psum | solution.py:118
  887.3 14.5 %fusion.40 = f32[4,1,40,64]{3,1,2,0:T(1,128)S(1)} fusion(f32[4,128,1,1]{1,2,3,0:T(1,128)S(1)} %bitcast.406, f32[4,40,64,128]{3,2,1,0:T(8,128)} %gather_fusion.18, f32[4,128]{1,0:T(4,128)S(1)} %get-tuple-element.106, f32[4,40,64]{2,1,0:T(8,128)S(1)} %broadcast_multiply_fusion, f32[4]{0:T(128)S(1)} %get-tuple-element.151, f32[4,40]{1,0:T(4,128)S(1)} %get-tuple-element.21, ...), kind=kOutput, calls=%fused_computation.69 | convolution fusion | flops 22282240 | bytes 5329556 | tf_op jit(solution)/shard_map/bhpn,bn->bhp/dot_general | solution.py:161
  915.0 8.1 select_dynamic-update-slice_fusion
  923.1 16.4 %copy.150 = f32[1,16,40,64,128]{4,3,2,1,0:T(8,128)} copy(f32[1,16,40,64,128]{4,3,2,1,0:T(8,128)} %bitcast.322) | data formatting | bytes 41943040
  942.7 8.1 bitcast_dynamic-update-slice_fusion
  950.8 22.7 %all-reduce.48.cloned.1.call-done = f32[16,1280]{1,0:T(8,128)} async-done(((f32[16,1280]{1,0:T(8,128)}), f32[16,1280]{1,0:T(8,128)}) %all-reduce.48.cloned.1.call-update) | async-done | bytes 81936
  (373 shorter events, 248.9 us)
Async XLA Ops:
  7.2 27.0 %copy-start = (bf16[1,18,3,2560]{3,2,1,0:T(4,128)(2,1)S(1)}, bf16[1,18,3,2560]{3,2,1,0:T(4,128)(2,1)}, u32[]{:S(2)}) copy-start(bf16[1,18,3,2560]{3,2,1,0:T(4,128)(2,1)} %param.29) | copy-start | bytes 829444
  7.2 17.8 %copy-start.2 = (bf16[1,84,1280]{2,1,0:T(8,128)(2,1)S(1)}, bf16[1,84,1280]{2,1,0:T(8,128)(2,1)}, u32[]{:S(2)}) copy-start(bf16[1,84,1280]{2,1,0:T(8,128)(2,1)} %param.26) | copy-start | bytes 645124
  7.2 26.7 %copy-start.4 = (f32[1,4,2560]{2,1,0:T(4,128)S(1)}, f32[1,4,2560]{2,1,0:T(4,128)}, u32[]{:S(2)}) copy-start(f32[1,4,2560]{2,1,0:T(4,128)} %param.27) | copy-start | bytes 122884
  7.2 26.8 %copy-start.12 = (s32[16]{0:T(128)S(1)}, s32[16]{0:T(128)}, u32[]{:S(2)}) copy-start(s32[16]{0:T(128)} %param.23) | copy-start | bytes 196
  7.2 26.8 %copy-start.7 = (s32[16]{0:T(128)S(1)}, s32[16]{0:T(128)}, u32[]{:S(2)}) copy-start(s32[16]{0:T(128)} %param.22) | copy-start | bytes 196
  7.2 27.6 %copy-start.3 = (bf16[1,18,3,256]{3,2,1,0:T(4,128)(2,1)S(1)}, bf16[1,18,3,256]{3,2,1,0:T(4,128)(2,1)}, u32[]{:S(2)}) copy-start(bf16[1,18,3,256]{3,2,1,0:T(4,128)(2,1)} %param.30) | copy-start | bytes 82948
  7.2 28.2 %copy-start.11 = (f32[1,4,256]{2,1,0:T(4,128)S(1)}, f32[1,4,256]{2,1,0:T(4,128)}, u32[]{:S(2)}) copy-start(f32[1,4,256]{2,1,0:T(4,128)} %param.28) | copy-start | bytes 12292
  7.2 40.6 %all-reduce.22.cloned.1.call-start = ((), (), s32[]{:S(2)}) async-start(), calls=%async_computation.21 | async-start | bytes 163840 | tf_op jit(solution)/shard_map/psum | solution.py:118
  30.6 16.5 %all-to-all-start = ((bf16[4,4,84]{2,1,0:T(4,128)(2,1)}), bf16[4,4,84]{2,1,0:T(4,128)(2,1)S(1)}, u32[]{:S(2)}, u32[]{:S(2)}) async-start(bf16[4,4,84]{2,1,0:T(4,128)(2,1)} %psum.147), calls=%async_computation | async-start | bytes 8192 | tf_op jit(solution)/shard_map/all_to_all | solution.py:126
  36.1 11.1 %copy-start.10 = (f32[1,2560]{1,0:T(1,128)S(1)}, f32[1,2560]{1,0:T(1,128)}, u32[]{:S(2)}) copy-start(f32[1,2560]{1,0:T(1,128)} %param.35) | copy-start | bytes 30724
  36.1 16.6 %copy-start.8 = (f32[1,40]{1,0:T(1,128)S(1)}, f32[1,40]{1,0:T(1,128)}, u32[]{:S(2)}) copy-start(f32[1,40]{1,0:T(1,128)} %param.32) | copy-start | bytes 484
  36.1 16.6 %copy-start.9 = (f32[1,40]{1,0:T(1,128)S(1)}, f32[1,40]{1,0:T(1,128)}, u32[]{:S(2)}) copy-start(f32[1,40]{1,0:T(1,128)} %param.33) | copy-start | bytes 484
  47.1 24.9 %copy-start.6 = (f32[1,40]{1,0:T(1,128)S(1)}, f32[1,40]{1,0:T(1,128)}, u32[]{:S(2)}) copy-start(f32[1,40]{1,0:T(1,128)} %param.34) | copy-start | bytes 484
  49.4 7.5 all-to-all-start.1
  72.1 24.7 %copy-start.13 = (u32[32]{0:T(128)S(1)}, u32[32]{0:T(128)}, u32[]{:S(2)}) copy-start(u32[32]{0:T(128)} %constant.157) | copy-start | bytes 388
  82.0 7.2 all-to-all-start.2
  85.2 39.1 %all-reduce.36.cloned.1.call-start = ((), (), s32[]{:S(2)}) async-start(), calls=%async_computation.28 | async-start | bytes 163840
  129.5 14.6 %collective-permute-start = (bf16[4,2560]{1,0:T(4,128)(2,1)S(1)}, bf16[4,2560]{1,0:T(4,128)(2,1)S(1)}, u32[]{:S(2)}, u32[]{:S(2)}) collective-permute-start(bf16[4,2560]{1,0:T(4,128)(2,1)S(1)} %all_gather.66), channel_id=1, source_target_pairs={{0,1},{1,2},{2,3},{4,5},{5,6},{6,7},{8,9},{9,10},{10,11},{12,13},{... | collective-permute-start | bytes 61448 | tf_op jit(solution)/shard_map/ppermute | solution.py:15
  155.3 8.8 all-to-all-start.3
  158.5 27.2 %all-reduce.24.cloned.1.call-start = ((), (), s32[]{:S(2)}) async-start(), calls=%async_computation.22 | async-start | bytes 163840 | tf_op jit(solution)/shard_map/psum | solution.py:118
  187.3 7.5 all-to-all-start.4
  190.6 68.1 %all-reduce.38.cloned.1.call-start = ((), (), s32[]{:S(2)}) async-start(), calls=%async_computation.29 | async-start | bytes 163840
  263.9 14.5 %collective-permute-start.1 = (bf16[4,2560]{1,0:T(4,128)(2,1)S(1)}, bf16[4,2560]{1,0:T(4,128)(2,1)S(1)}, u32[]{:S(2)}, u32[]{:S(2)}) collective-permute-start(bf16[4,2560]{1,0:T(4,128)(2,1)S(1)} %all_gather.69), channel_id=1, source_target_pairs={{0,1},{1,2},{2,3},{4,5},{5,6},{6,7},{8,9},{9,10},{10,11},{12,13},{... | collective-permute-start | bytes 61448 | tf_op jit(solution)/shard_map/ppermute | solution.py:15
  289.5 8.6 all-to-all-start.6
  292.8 27.0 %all-reduce.26.cloned.1.call-start = ((), (), s32[]{:S(2)}) async-start(), calls=%async_computation.23 | async-start | bytes 163840 | tf_op jit(solution)/shard_map/psum | solution.py:118
  321.4 7.5 all-to-all-start.7
  324.7 68.1 %all-reduce.40.cloned.1.call-start = ((), (), s32[]{:S(2)}) async-start(), calls=%async_computation.30 | async-start | bytes 163840
  397.9 14.4 %collective-permute-start.2 = (bf16[4,2560]{1,0:T(4,128)(2,1)S(1)}, bf16[4,2560]{1,0:T(4,128)(2,1)S(1)}, u32[]{:S(2)}, u32[]{:S(2)}) collective-permute-start(bf16[4,2560]{1,0:T(4,128)(2,1)S(1)} %all_gather.72), channel_id=1, source_target_pairs={{0,1},{1,2},{2,3},{4,5},{5,6},{6,7},{8,9},{9,10},{10,11},{12,13},{... | collective-permute-start | bytes 61448 | tf_op jit(solution)/shard_map/ppermute | solution.py:15
  423.4 8.6 all-to-all-start.9
  426.7 27.0 %all-reduce.28.cloned.1.call-start = ((), (), s32[]{:S(2)}) async-start(), calls=%async_computation.24 | async-start | bytes 163840 | tf_op jit(solution)/shard_map/psum | solution.py:118
  455.3 7.5 all-to-all-start.10
  458.6 68.3 %all-reduce.42.cloned.1.call-start = ((), (), s32[]{:S(2)}) async-start(), calls=%async_computation.31 | async-start | bytes 163840
  532.0 14.4 %collective-permute-start.3 = (bf16[4,2560]{1,0:T(4,128)(2,1)S(1)}, bf16[4,2560]{1,0:T(4,128)(2,1)S(1)}, u32[]{:S(2)}, u32[]{:S(2)}) collective-permute-start(bf16[4,2560]{1,0:T(4,128)(2,1)S(1)} %all_gather.75), channel_id=1, source_target_pairs={{0,1},{1,2},{2,3},{4,5},{5,6},{6,7},{8,9},{9,10},{10,11},{12,13},{... | collective-permute-start | bytes 61448 | tf_op jit(solution)/shard_map/ppermute | solution.py:15
  557.6 8.6 all-to-all-start.12
  560.9 27.0 %all-reduce.30.cloned.1.call-start = ((), (), s32[]{:S(2)}) async-start(), calls=%async_computation.25 | async-start | bytes 163840 | tf_op jit(solution)/shard_map/psum | solution.py:118
  589.5 7.5 all-to-all-start.13
  622.0 25.2 %all-to-all-start.14 = ((bf16[4,4,1280]{2,0,1:T(4,128)(2,1)}), bf16[4,4,1280]{2,0,1:T(4,128)(2,1)S(1)}, u32[]{:S(2)}, u32[]{:S(2)}) async-start(bf16[4,4,1280]{2,0,1:T(4,128)(2,1)} %bitcast.69), calls=%async_computation.14 | async-start | bytes 81920 | tf_op jit(solution)/shard_map/all_to_all | solution.py:172
  625.3 56.1 %all-reduce.44.cloned.1.call-start = ((), (), s32[]{:S(2)}) async-start(), calls=%async_computation.32 | async-start | bytes 163840
  647.2 12.9 %slice-start = ((s8[5242880]{0:T(1024)(128)(4,1)}), s8[1048576]{0:T(1024)(128)(4,1)S(1)}, s32[]{:S(2)}) async-start(s8[5242880]{0:T(1024)(128)(4,1)} %bitcast.330), calls=%async_computation.35 | async-start | bytes 2097152
  650.5 9.7 slice-start.1
  686.5 11.7 %collective-permute-start.4 = (bf16[4,2560]{1,0:T(4,128)(2,1)S(1)}, bf16[4,2560]{1,0:T(4,128)(2,1)S(1)}, u32[]{:S(2)}, u32[]{:S(2)}) collective-permute-start(bf16[4,2560]{1,0:T(4,128)(2,1)S(1)} %all_gather.78), channel_id=1, source_target_pairs={{0,1},{1,2},{2,3},{4,5},{5,6},{6,7},{8,9},{9,10},{10,11},{12,13},{... | collective-permute-start | bytes 61448 | tf_op jit(solution)/shard_map/ppermute | solution.py:15
  709.4 8.6 all-to-all-start.15
  712.6 27.1 %all-reduce.32.cloned.1.call-start = ((), (), s32[]{:S(2)}) async-start(), calls=%async_computation.26 | async-start | bytes 163840 | tf_op jit(solution)/shard_map/psum | solution.py:118
  741.3 7.5 all-to-all-start.16
  773.8 11.4 %all-to-all-start.17 = ((bf16[4,4,1280]{2,0,1:T(4,128)(2,1)}), bf16[4,4,1280]{2,0,1:T(4,128)(2,1)S(1)}, u32[]{:S(2)}, u32[]{:S(2)}) async-start(bf16[4,4,1280]{2,0,1:T(4,128)(2,1)} %bitcast.81), calls=%async_computation.17 | async-start | bytes 81920 | tf_op jit(solution)/shard_map/all_to_all | solution.py:172
  777.1 42.2 %all-reduce.46.cloned.1.call-start = ((), (), s32[]{:S(2)}) async-start(), calls=%async_computation.33 | async-start | bytes 163840
  824.5 11.5 %collective-permute-start.5 = (bf16[4,2560]{1,0:T(4,128)(2,1)S(1)}, bf16[4,2560]{1,0:T(4,128)(2,1)S(1)}, u32[]{:S(2)}, u32[]{:S(2)}) collective-permute-start(bf16[4,2560]{1,0:T(4,128)(2,1)S(1)} %all_gather.81), channel_id=1, source_target_pairs={{0,1},{1,2},{2,3},{4,5},{5,6},{6,7},{8,9},{9,10},{10,11},{12,13},{... | collective-permute-start | bytes 61448 | tf_op jit(solution)/shard_map/ppermute | solution.py:15
  847.1 8.6 all-to-all-start.18
  850.4 27.0 %all-reduce.34.cloned.1.call-start = ((), (), s32[]{:S(2)}) async-start(), calls=%async_computation.27 | async-start | bytes 163840 | tf_op jit(solution)/shard_map/psum | solution.py:118
  878.9 7.7 all-to-all-start.19
  911.7 27.8 %all-to-all-start.20 = ((bf16[4,4,1280]{2,0,1:T(4,128)(2,1)}), bf16[4,4,1280]{2,0,1:T(4,128)(2,1)S(1)}, u32[]{:S(2)}, u32[]{:S(2)}) async-start(bf16[4,4,1280]{2,0,1:T(4,128)(2,1)} %bitcast.94), calls=%async_computation.20 | async-start | bytes 81920 | tf_op jit(solution)/shard_map/all_to_all | solution.py:172
  915.0 58.5 %all-reduce.48.cloned.1.call-start = ((), (), s32[]{:S(2)}) async-start(), calls=%async_computation.34 | async-start | bytes 163840
  942.7 32.2 %copy-start.1 = (bf16[1,18,3,2560]{3,2,1,0:T(4,128)(2,1)S(1)}, bf16[1,18,3,2560]{3,2,1,0:T(4,128)(2,1)}, u32[]{:S(2)}) copy-start(bf16[1,18,3,2560]{3,2,1,0:T(4,128)(2,1)} %param.29) | copy-start | bytes 829444
  974.3 0.6 copy-start.5
Sparse Core Ops, SparseCore 0:
  25.0 22.7 all-reduce.21
  92.5 31.8 all-reduce.35
  164.2 21.4 all-reduce.23
  229.3 29.3 all-reduce.37
  298.3 21.4 all-reduce.25
  363.4 29.3 all-reduce.39
  432.2 21.4 all-reduce.27
  497.5 29.3 all-reduce.41
  566.4 21.4 all-reduce.29
  650.6 30.7 all-reduce.43
  718.1 21.5 all-reduce.31
  788.4 30.7 all-reduce.45
  855.9 21.4 all-reduce.33
  942.8 30.6 all-reduce.47
where the time goes:
time: 994 us; the launch traced here: 982 us
  waiting for transfers between devices  336 us (34%)
  blocking collectives  193 us (19%)
  matrix products  161 us (16%)
  local copies, waits for them, and re-layouts  129 us (13%)
  starting transfers between devices  80.8 us (8%)
  other arithmetic  65.8 us (7%)
  between operations  16.3 us (2%)
    unnamed x21, waiting for transfers between devices  178 us
    psum x7, waiting for transfers between devices, local(): lax.psum(zx_part.astype(jnp.bfloat16), 'mp').astype(jnp.float32)  130 us
    dot_general x7, matrix products, local(): jnp.einsum('bhpn,bn->bhp', new_state, conv_c, precision=lax.Precision.HIG...  101 us
    gather x7, local copies, waits for them, and re-layouts, local(): jnp.take(state_pool[0], rows_slot, axis=0) * alive[:, None, None, None]  76.5 us
    dynamic_update_slice x7, other arithmetic, local(): lax.dynamic_update_slice_in_dim(state_buffer, jnp.where(in_range, new_sta...  52.3 us
    psum x7, blocking collectives, local(): lax.psum(small_part.astype(jnp.bfloat16), 'mp').astype(jnp.float32)  38.8 us
    dot_general x7, matrix products, local(): jnp.einsum('rf,kcf->rkc', rows_all, w_zxo[0, :2], preferred_element_type=...  37.1 us
    all_gather x7, blocking collectives, local(): rows_all = lax.all_gather(normed_share, 'dp', axis=0, tiled=True)  36.4 us
  transfers between devices with their start and end apart: 38, of which 22 were waited for; matrix products, arithmetic and copies ran while one was open for 20% of the time, Pallas kernels for 0%

commit v1 on v0

v1 whole, which is shorter than its diff:
```python
import functools

import jax
import jax.numpy as jnp
from jax import lax
from jax.experimental import pallas as pl
from jax.experimental.pallas import tpu as pltpu
from jax.sharding import PartitionSpec as P

epsilon = 1e-05
LANES = 128
SUBLANES = 8
MEBI = 1 << 20
CHUNKS = 4


def padded(width):
    return -(-width // LANES) * LANES


def in_vmem(count):
    return [pl.BlockSpec(memory_space=pltpu.VMEM)] * count


def in_smem(count):
    return [pl.BlockSpec(memory_space=pltpu.SMEM)] * count


def lanes_of(shape):
    return lax.broadcasted_iota(jnp.int32, shape, 1)


def two_parts(column, lane):
    high = column.astype(jnp.bfloat16).astype(jnp.float32)
    low = column - high
    return jnp.where(lane == 0, high, jnp.where(lane == 1, low, 0.0))


def against(inputs, weights):
    return lax.dot_general(
        inputs, weights, (((1,), (1,)), ((), ())), preferred_element_type=jnp.float32
    )


def load_kernel(
    pieces,
    slots_ref,
    lengths_ref,
    pool_ref,
    w_ref,
    conv_x_ref,
    conv_bc_ref,
    table_ref,
    heads_ref,
    *refs,
):
    held_refs = refs[:CHUNKS]
    (
    w_out_ref,
    past_x_ref,
    past_bc_ref,
    wide_ref,
    head_ref,
    now_bc_ref,
    alive_ref,
    history_x,
    history_bc,
    sems,
    w_sems,
    small_sems,
    ) = refs[CHUNKS:]
    chunk, heads = held_refs[0].shape[:2]
    rows = chunk * CHUNKS
    chan = past_x_ref.shape[1]
    each = heads // pieces

    def copies(c, i):
        for k in range(pieces):
            part = pl.ds(k * each, each)
            yield pltpu.make_async_copy(
                pool_ref.at[0, slots_ref[c * chunk + i], part],
                held_refs[c].at[i, part],
                sems.at[c * chunk + i, k],
            )

    small_copies = [
        pltpu.make_async_copy(source, target, small_sems.at[k])
        for k, (source, target) in enumerate(
            (
                (conv_x_ref, history_x),
                (conv_bc_ref, history_bc),
            )
        )
    ]
    w_copies = [
        pltpu.make_async_copy(w_ref.at[0, k], w_out_ref.at[k], w_sems.at[k])
        for k in range(w_out_ref.shape[0])
    ]
    for copy in small_copies + w_copies:
        copy.start()

    for c in range(CHUNKS):

        def start(i, carry):
            for copy in copies(c, i):
                copy.start()
            return carry

        lax.fori_loop(0, chunk, start, 0)
    for copy in small_copies:
        copy.wait()
    alive = jnp.zeros(alive_ref.shape, jnp.float32)
    row = lax.broadcasted_iota(jnp.int32, alive_ref.shape, 0)
    for i in range(rows):
        length = lengths_ref[i]
        for history_ref, above, past_ref in (
            (history_x, 0, past_x_ref),
            (history_bc, 4, past_bc_ref),
        ):
            history = history_ref[0, slots_ref[i]].astype(jnp.float32)
            taps = history.shape[0]
            tap = lax.broadcasted_iota(jnp.int32, (taps, 1), 0)
            known = (length >= taps - tap).astype(jnp.float32)
            past_ref[i : i + 1, :] = jnp.sum(
                history * known * table_ref[above : above + taps, : history.shape[1]],
                axis=0, keepdims=True
            )
        alive = jnp.where(row == i, (length > 0).astype(jnp.float32), alive)
    alive_ref[...] = alive
    onto = lax.broadcasted_iota(jnp.int32, (heads, chan), 0)
    onto = (onto == lanes_of((heads, chan)) // (chan // heads)).astype(jnp.float32)
    for k in range(3):
        wide = jnp.dot(
            jnp.broadcast_to(heads_ref[k : k + 1, :], (SUBLANES, heads)),
            onto,
            precision=lax.Precision.HIGHEST,
            preferred_element_type=jnp.float32,
        )
        wide_ref[k : k + 1, :] = wide[:1]
    wide_ref[3:4, :] = table_ref[8:9, :]
    wide_ref[4:5, :] = table_ref[3:4, :]
    now_bc_ref[...] = table_ref[7:8, : now_bc_ref.shape[1]]
    head_ref[...] = heads_ref[:2, :]
    for copy in w_copies:
        copy.wait()
    for c in range(CHUNKS):

        def wait(i, carry):
            for copy in copies(c, i):
                copy.wait()
            return carry

        lax.fori_loop(0, chunk, wait, 0)


def load(slots, lengths, pool, w, conv_x, conv_bc, table, by_head):
    rows = slots.shape[0]
    heads, head_size, width = pool.shape[2:]
    pieces = 2 if heads % 2 == 0 else 1
    chan = conv_x.shape[3]
    bc_width = conv_bc.shape[3]
    made = rows * heads * head_size * width * 4 + w.size * 2
    return pl.pallas_call(
        functools.partial(load_kernel, pieces),
        out_shape=[
            *[jax.ShapeDtypeStruct((rows // CHUNKS, heads, head_size, width), jnp.float32)] * CHUNKS,
            jax.ShapeDtypeStruct(w.shape[1:], jnp.bfloat16),
            jax.ShapeDtypeStruct((rows, chan), jnp.float32),
            jax.ShapeDtypeStruct((rows, bc_width), jnp.float32),
            jax.ShapeDtypeStruct((5, chan), jnp.float32),
            jax.ShapeDtypeStruct((2, heads), jnp.float32),
            jax.ShapeDtypeStruct((1, bc_width), jnp.float32),
            jax.ShapeDtypeStruct((rows, LANES), jnp.float32),
        ],
        in_specs=in_smem(2) + [pl.BlockSpec(memory_space=pltpu.HBM)] * 4 + in_vmem(2),
        out_specs=in_vmem(7 + CHUNKS),
        scratch_shapes=[
            pltpu.VMEM(conv_x.shape, conv_x.dtype),
            pltpu.VMEM(conv_bc.shape, conv_bc.dtype),
            pltpu.SemaphoreType.DMA((rows, pieces)),
            pltpu.SemaphoreType.DMA((w.shape[1],)),
            pltpu.SemaphoreType.DMA((2,)),
        ],
        compiler_params=pltpu.CompilerParams(vmem_limit_bytes=5 * MEBI),
        cost_estimate=pl.CostEstimate(
            flops=rows * heads * head_size * width * 16, bytes_accessed=made, transcendentals=0
        ),
        name="load",
    )(slots, lengths, pool, w, conv_x, conv_bc, table, by_head)


def for_each_part(target, parts, act):
    if parts == 1:
        act(0)
        return
    for part in range(parts):
        pl.when(target % parts == part)(functools.partial(act, part))


def row_of(target, parts, group, seq_dev, mine):
    block = target // parts
    return pl.multiple_of((((block % group) ^ mine) * 2 + block // group) * seq_dev, seq_dev)


def project_kernel(
    parts, seq_dev, sharers, group, blocks, place_ref, gain_ref, w_ref, *refs
):
    small_refs = refs[:sharers]
    hidden_refs = refs[sharers : sharers + group]
    *out_refs, scaled_ref, held = refs[sharers + group :]
    chan = w_ref.shape[1]
    piece = chan // parts
    wide = 2 * chan
    source, dp_index = place_ref[2], place_ref[3]
    lane = lanes_of((hidden_refs[0].shape[0], LANES))
    for k, hidden_ref in enumerate(hidden_refs):
        hidden = hidden_ref[...].astype(jnp.float32)
        rows = slice(k * hidden.shape[0], (k + 1) * hidden.shape[0])
        scaled_ref[rows, :] = (hidden * gain_ref[...]).astype(jnp.bfloat16)
        square = jnp.sum(hidden * hidden, axis=1, keepdims=True)
        held[rows, held.shape[1] - LANES :] = two_parts(square, lane).astype(jnp.bfloat16)
    scaled = scaled_ref[...]
    held[:, :chan] = against(scaled, w_ref[1]).astype(jnp.bfloat16)
    held[:, chan:wide] = against(scaled, w_ref[0]).astype(jnp.bfloat16)
    small_width = held.shape[1] - LANES - wide
    tail = jnp.zeros((scaled.shape[0], small_width), jnp.float32)
    for r, small_ref in enumerate(small_refs):
        count = small_ref.shape[0]
        block = ((dp_index // blocks) ^ r) * blocks + dp_index % blocks
        onto = lax.broadcasted_iota(jnp.int32, (count, small_width), 0) + block * count
        onto = (onto == lanes_of((count, small_width))).astype(jnp.bfloat16)
        small = against(scaled, small_ref[...]).astype(jnp.bfloat16)
        tail = tail + jnp.dot(small, onto, preferred_element_type=jnp.float32)
    held[:, wide : wide + small_width] = tail.astype(jnp.bfloat16)
    for r, out_ref in enumerate(out_refs):
        target = source ^ r
        rows = pl.ds(row_of(target, parts, group, seq_dev, dp_index % group), seq_dev)

        def fill(first):
            out_ref[:, :piece] = held[rows, first : first + piece]
            out_ref[:, piece : 2 * piece] = held[rows, chan + first : chan + first + piece]

        for_each_part(target, parts, lambda part: fill(part * piece))
        out_ref[:, 2 * piece :] = held[rows, wide:]


def project(parts, rounds, seq_dev, blocks, small_width, place, gain, w, smalls, hiddens):
    chan, share = w.shape[1:]
    width = 2 * chan // parts + small_width + LANES
    rows = hiddens[0].shape[0] * len(hiddens)
    return pl.pallas_call(
        functools.partial(project_kernel, parts, seq_dev, len(smalls), len(hiddens), blocks),
        out_shape=[jax.ShapeDtypeStruct((seq_dev, width), jnp.bfloat16)] * rounds,
        in_specs=in_smem(1) + in_vmem(2 + len(smalls) + len(hiddens)),
        out_specs=in_vmem(rounds),
        scratch_shapes=[
            pltpu.VMEM((rows, share), jnp.bfloat16),
            pltpu.VMEM((rows, 2 * chan + small_width + LANES), jnp.bfloat16),
        ],
        compiler_params=pltpu.CompilerParams(vmem_limit_bytes=6 * MEBI),
        cost_estimate=pl.CostEstimate(
            flops=2 * rows * share * (2 * chan + small_width),
            bytes_accessed=2 * share * (2 * chan + small_width),
            transcendentals=0,
        ),
        name="project",
    )(place, gain, w, *smalls, *hiddens)


def mix_kernel(
    tick,
    rounds,
    parts,
    mp_count,
    model_width,
    heads,
    place_ref,
    past_x_ref,
    past_bc_ref,
    now_bc_ref,
    wide_ref,
    head_ref,
    alive_ref,
    *refs,
):
    held_refs = refs[:CHUNKS]
    refs = refs[CHUNKS:]
    got_refs = refs[:rounds]
    before_refs = refs[rounds : rounds + 3 * (tick > 0)]
    refs = refs[rounds + len(before_refs) :]
    out_refs = refs[:rounds]
    decay_ref, x_ref, b_ref, c_ref, read_ref, gated_ref, inner_ref, gate_ref = refs[rounds:]

    def keep(k, ref, value):
        if tick > 0:
            value = jnp.where(place_ref[4] == tick, value, before_refs[k][...])
        ref[...] = value

    seq_dev, chan = past_x_ref.shape
    head_size = chan // heads
    bc_width = past_bc_ref.shape[1]
    blocks = max(1, rounds // mp_count)
    piece = chan // blocks
    target = place_ref[0]
    mp_index = place_ref[1]
    tail_width = got_refs[0].shape[1] - 2 * piece

    for j in range(blocks):
        both = jnp.zeros((seq_dev, 2 * piece), jnp.float32)
        for r, got_ref in enumerate(got_refs):
            chosen = ((target ^ r) % blocks == j).astype(jnp.float32)
            both = both + chosen * got_ref[:, : 2 * piece].astype(jnp.float32)
        inner_ref[:, j * piece : (j + 1) * piece] = both[:, :piece]
        gate_ref[:, j * piece : (j + 1) * piece] = both[:, piece:]
    tail = jnp.zeros((seq_dev, tail_width), jnp.float32)
    for got_ref in got_refs:
        tail = tail + got_ref[:, 2 * piece :].astype(jnp.float32)
    square = jnp.sum(tail[:, tail_width - LANES :], axis=1, keepdims=True) / blocks
    scale = lax.rsqrt(square / model_width + epsilon)
    conv_bc = jax.nn.silu(past_bc_ref[...] + tail[:, :bc_width] * scale * now_bc_ref[...])
    conv_b = conv_bc[:, : bc_width // 2]
    conv_c = conv_bc[:, bc_width // 2 :]
    keep(2, b_ref, conv_b)
    c_ref[...] = conv_c
    read_ref[...] = jnp.zeros_like(read_ref)
    group = min(heads, 8)
    while group and (heads % group or group * head_size % LANES):
        group -= 1
    group = group or heads

    chunk = seq_dev // CHUNKS

    def work(c, at, carry):
        i = c * chunk + at
        c_rows = jnp.broadcast_to(c_ref[pl.ds(i, 1), :], (SUBLANES, conv_c.shape[1]))
        c_rows = c_rows.astype(jnp.bfloat16)
        found = []
        for first in range(0, heads, group):
            state = held_refs[c][at, first : first + group]
            state = state.reshape(group * head_size, state.shape[2]).astype(jnp.bfloat16)
            found.append(against(c_rows, state))
        tile = pl.ds(pl.multiple_of(i // SUBLANES * SUBLANES, SUBLANES), SUBLANES)
        width = group * head_size
        mine = lax.broadcasted_iota(jnp.int32, (SUBLANES, width), 0) == i % SUBLANES
        for k, y in enumerate(found):
            columns = slice(k * width, (k + 1) * width)
            read_ref[tile, columns] = jnp.where(mine, y, read_ref[tile, columns])
        return carry

    for c in range(CHUNKS):
        lax.fori_loop(0, chunk, functools.partial(work, c), 0)

    raw = tail[:, bc_width : tail_width - LANES] * scale
    raw_width = raw.shape[1]
    pick = lambda shape, per: (
        lax.broadcasted_iota(jnp.int32, shape, 0) == mp_index * heads + lanes_of(shape) // per
    ).astype(jnp.float32)
    chosen = lambda per, width: jnp.dot(
        raw,
        pick((raw_width, width), per),
        precision=lax.Precision.HIGHEST,
        preferred_element_type=jnp.float32,
    )
    softplus = lambda v: jnp.maximum(v, 0.0) + jnp.log1p(jnp.exp(-jnp.abs(v)))
    alive = alive_ref[:, :1]
    step_heads = softplus(chosen(1, heads) + head_ref[0:1, :])
    keep(0, decay_ref, jnp.exp(-step_heads * head_ref[1:2, :]) * alive)
    step = softplus(chosen(head_size, chan) + wide_ref[0:1, :])
    decay = jnp.exp(-step * wide_ref[1:2, :]) * alive
    conv_x = jax.nn.silu(past_x_ref[...] + inner_ref[...] * scale * wide_ref[4:5, :])
    x_step = conv_x * step
    keep(1, x_ref, x_step)
    cross = jnp.sum(conv_b * conv_c, axis=1, keepdims=True)
    y = decay * read_ref[...] + x_step * cross + wide_ref[2:3, :] * conv_x
    gated = y * jax.nn.silu(gate_ref[...] * scale)
    square = jnp.sum(gated * gated, axis=1, keepdims=True)
    gated_ref[...] = (gated * wide_ref[3:4, :]).astype(jnp.bfloat16)
    out_tail = two_parts(square, lanes_of((seq_dev, LANES))).astype(jnp.bfloat16)
    for r, out_ref in enumerate(out_refs):
        first = pl.multiple_of((target ^ r) % blocks * piece, LANES) if blocks > 1 else 0
        out_ref[:, :piece] = gated_ref[:, pl.ds(first, piece)]
        out_ref[:, piece:] = out_tail


def mix(
    tick, parts, mp_count, model_width, place, past_x, past_bc, now_bc, wide, head, alive, held,
    got, before,
):
    rounds = len(got)
    seq_dev, chan = past_x.shape
    heads = head.shape[1]
    piece = chan // max(1, rounds // mp_count)
    state_size = held[0].shape[3]
    return pl.pallas_call(
        functools.partial(mix_kernel, tick, rounds, parts, mp_count, model_width, heads),
        out_shape=[jax.ShapeDtypeStruct((seq_dev, piece + LANES), jnp.bfloat16)] * rounds
        + [
            jax.ShapeDtypeStruct((seq_dev, heads), jnp.float32),
            jax.ShapeDtypeStruct((seq_dev, chan), jnp.float32),
            jax.ShapeDtypeStruct((seq_dev, state_size), jnp.float32),
        ],
        in_specs=in_smem(1) + in_vmem(6 + CHUNKS + rounds + len(before)),
        out_specs=in_vmem(rounds + 3),
        scratch_shapes=[
            pltpu.VMEM((seq_dev, state_size), jnp.float32),
            pltpu.VMEM((seq_dev, chan), jnp.float32),
            pltpu.VMEM((seq_dev, chan), jnp.bfloat16),
            pltpu.VMEM((seq_dev, chan), jnp.float32),
            pltpu.VMEM((seq_dev, chan), jnp.float32),
        ],
        compiler_params=pltpu.CompilerParams(vmem_limit_bytes=10 * MEBI),
        cost_estimate=pl.CostEstimate(
            flops=16 * seq_dev * chan * state_size,
            bytes_accessed=seq_dev * chan * state_size * 4,
            transcendentals=0,
        ),
        name="mix",
    )(place, past_x, past_bc, now_bc, wide, head, alive, *held, *got, *before)


def finish_kernel(rounds, parts, seq_dev, group, place_ref, w_ref, *refs):
    got_refs = refs[:rounds]
    out_refs = refs[rounds : rounds + group]
    rows_ref, square_ref = refs[rounds + group :]
    piece = got_refs[0].shape[1] - LANES
    square_ref[...] = jnp.zeros_like(square_ref)
    for r, got_ref in enumerate(got_refs):
        target = place_ref[2] ^ r
        rows = pl.ds(row_of(target, parts, group, seq_dev, place_ref[3] % group), seq_dev)

        def fill(first):
            rows_ref[rows, first : first + piece] = got_ref[:, :piece]

        for_each_part(target, parts, lambda part: fill(part * piece))
        square_ref[rows, :] += got_ref[:, piece:].astype(jnp.float32)
    square = jnp.sum(square_ref[...], axis=1, keepdims=True)
    tail = two_parts(square, lanes_of(square_ref.shape)).astype(jnp.bfloat16)
    partial = jnp.dot(rows_ref[...], w_ref[2], preferred_element_type=jnp.float32)
    partial = partial.astype(jnp.bfloat16)
    for k, out_ref in enumerate(out_refs):
        rows = slice(2 * seq_dev * k, 2 * seq_dev * (k + 1))
        out_ref[:, :LANES] = tail[rows]
        out_ref[:, LANES:] = partial[rows]


def finish(parts, group, place, w, got):
    rounds = len(got)
    chan, share = w.shape[1:]
    seq_dev = got[0].shape[0]
    seq_all = 2 * seq_dev * group
    return pl.pallas_call(
        functools.partial(finish_kernel, rounds, parts, seq_dev, group),
        out_shape=[jax.ShapeDtypeStruct((2 * seq_dev, LANES + share), jnp.bfloat16)] * group,
        in_specs=in_smem(1) + in_vmem(1 + rounds),
        out_specs=in_vmem(group),
        scratch_shapes=[
            pltpu.VMEM((seq_all, chan), jnp.bfloat16),
            pltpu.VMEM((seq_all, LANES), jnp.float32),
        ],
        compiler_params=pltpu.CompilerParams(vmem_limit_bytes=6 * MEBI),
        cost_estimate=pl.CostEstimate(
            flops=2 * seq_all * chan * share, bytes_accessed=2 * chan * share, transcendentals=0
        ),
        name="finish",
    )(place, w, *got)


def settle_kernel(tick, seq_dev, group, blocks, chan_total, place_ref, mine_ref, met_ref, old_ref, *refs):
    *before_refs, hidden_ref, own_ref = refs
    total = mine_ref[...].astype(jnp.float32) + met_ref[...].astype(jnp.float32)
    square = jnp.sum(total[:, :LANES], axis=1, keepdims=True) / blocks
    scale = lax.rsqrt(square / chan_total + epsilon)
    hidden = old_ref[...].astype(jnp.float32) + total[:, LANES:] * scale
    hidden_ref[...] = hidden.astype(jnp.bfloat16)
    first = pl.multiple_of(place_ref[3] // group * seq_dev, seq_dev)
    own = hidden_ref[pl.ds(first, seq_dev), :]
    for before_ref in before_refs:
        own = jnp.where(place_ref[4] == tick, own, before_ref[...])
    own_ref[...] = own


def settle(tick, group, blocks, chan_total, place, mine, met, old, before):
    rows, share = old.shape
    return pl.pallas_call(
        functools.partial(settle_kernel, tick, rows // 2, group, blocks, chan_total),
        out_shape=[
            jax.ShapeDtypeStruct((rows, share), jnp.bfloat16),
            jax.ShapeDtypeStruct((rows // 2, share), jnp.bfloat16),
        ],
        in_specs=in_smem(1) + in_vmem(3 + len(before)),
        out_specs=in_vmem(2),
        compiler_params=pltpu.CompilerParams(vmem_limit_bytes=4 * MEBI),
        cost_estimate=pl.CostEstimate(flops=rows * share * 8, bytes_accessed=rows * share * 10, transcendentals=0),
        name="settle",
    )(place, mine, met, old, *before)


def write_kernel(decay_ref, x_ref, b_ref, *refs):
    states_refs = refs[:CHUNKS]
    out_ref, held, sems = refs[CHUNKS:]
    rows, heads, head_size, width = held.shape
    together = LANES // head_size

    def copy_out(i):
        return pltpu.make_async_copy(held.at[i], out_ref.at[0, i], sems.at[i])

    chunk = rows // CHUNKS

    def work(c, at, carry):
        i = c * chunk + at
        b_rows = jnp.broadcast_to(b_ref[pl.ds(i, 1), :], (LANES, width))
        tile = pl.ds(pl.multiple_of(i // SUBLANES * SUBLANES, SUBLANES), SUBLANES)
        for first in range(0, heads, together):
            count = min(together, heads - first)
            columns = slice(first * head_size, (first + count) * head_size)
            chosen = lax.broadcasted_iota(jnp.int32, (SUBLANES, count * head_size), 0) == i % SUBLANES
            x_row = jnp.sum(jnp.where(chosen, x_ref[tile, columns], 0.0), axis=0, keepdims=True)
            x_rows = jnp.broadcast_to(x_row, (LANES, count * head_size))
            added = x_rows.T * b_rows[: count * head_size]
            for k in range(count):
                held[i, first + k] = (
                    states_refs[c][at, first + k] * decay_ref[i, first + k]
                    + added[k * head_size : (k + 1) * head_size]
                )
        copy_out(i).start()
        return carry

    def end(i, carry):
        copy_out(i).wait()
        return carry

    for c in range(CHUNKS):
        lax.fori_loop(0, chunk, functools.partial(work, c), 0)
    lax.fori_loop(0, rows, end, 0)


def write_states(decay, x, b, states):
    chunk, heads, head_size, width = states[0].shape
    rows = chunk * len(states)
    return pl.pallas_call(
        write_kernel,
        out_shape=jax.ShapeDtypeStruct((1, rows, heads, head_size, width), jnp.float32),
        in_specs=in_smem(1) + in_vmem(2 + CHUNKS),
        out_specs=pl.BlockSpec(memory_space=pl.ANY),
        scratch_shapes=[
            pltpu.VMEM((rows, heads, head_size, width), jnp.float32),
            pltpu.SemaphoreType.DMA((rows,)),
        ],
        compiler_params=pltpu.CompilerParams(
            vmem_limit_bytes=rows * heads * head_size * width * 4 + 3 * MEBI
        ),
        cost_estimate=pl.CostEstimate(
            flops=16 * rows * heads * head_size * width,
            bytes_accessed=rows * heads * head_size * width * 8,
            transcendentals=0,
        ),
        name="write_states",
    )(decay, x, b, *states)


def local(
    hidden_in,
    lengths,
    slots,
    norm_gain,
    w_zxo,
    w_bcdt,
    conv_x_weight,
    conv_bc_weight,
    conv_x_pool,
    conv_bc_pool,
    state_pool,
    a_rate,
    dt_bias,
    skip_gain,
    gate_gain,
):
    section_index = lax.axis_index("section")
    section_count = lax.axis_size("section")
    mp_index = lax.axis_index("mp")
    mp_count = lax.axis_size("mp")
    dp_index = lax.axis_index("dp")
    dp_count = lax.axis_size("dp")
    seq_dev, model_share = hidden_in.shape
    seq_all = seq_dev * dp_count
    model_width = norm_gain.shape[1]
    heads_dev = a_rate.shape[1]
    head_size = state_pool.shape[3]
    chan_dev = heads_dev * head_size
    slots_dev = state_pool.shape[1]
    bc_width = conv_bc_weight.shape[2]
    small_dev = w_bcdt.shape[1]
    small_all = small_dev * dp_count
    chan_saved = w_zxo.shape[2]
    chan_total = chan_saved * dp_count
    small_pad = bc_width + padded(small_all - bc_width)

    blocks = max(1, dp_count // mp_count)
    parts = max(1, mp_count // dp_count)
    rounds = dp_count * parts

    def places():
        for d in range(dp_count):
            for m in range(mp_count):
                yield d, m, d // blocks, m * blocks + d % blocks

    def forward_pairs(r):
        pairs = []
        for d, m, group, source in places():
            target = source ^ r
            to_d = target // parts
            to_m = group * parts + target % parts
            pairs.append((d * mp_count + m, to_d * mp_count + to_m))
        return pairs

    def to_heads(of_round):
        return [
            lax.ppermute(piece, ("dp", "mp"), forward_pairs(r)) for r, piece in enumerate(of_round)
        ]

    def to_blocks(of_round):
        return [
            lax.ppermute(piece, ("dp", "mp"), [(b, a) for a, b in forward_pairs(r)])
            for r, piece in enumerate(of_round)
        ]

    group = dp_count // 2
    own_part = dp_index % group

    def across(array, by):
        return lax.ppermute(array, "dp", [(d, d ^ by) for d in range(dp_count)])

    def with_others(array):
        return [array] + [across(array, r) for r in range(1, group)]

    source_index = mp_index * blocks + dp_index % blocks
    target_index = dp_index * parts + mp_index % parts
    place = jnp.stack([target_index, mp_index, source_index, dp_index, section_index]).astype(jnp.int32)

    met = across(hidden_in, group)
    first_half = dp_index < group
    hidden = jnp.concatenate(
        [jnp.where(first_half, hidden_in, met), jnp.where(first_half, met, hidden_in)], axis=0
    )
    smalls = [w_bcdt[0]] + [across(w_bcdt[0], blocks * r) for r in range(1, dp_count // blocks)]
    gain_share = lax.dynamic_slice_in_dim(norm_gain, mp_index * model_share, model_share, 1)
    table = jnp.concatenate(
        [
            conv_x_weight[0],
            jnp.pad(conv_bc_weight[0], ((0, 0), (0, chan_dev - bc_width))),
            gate_gain,
        ],
        axis=0,
    )
    *held, w, past_x, past_bc, wide, head, now_bc, alive = load(
        slots - dp_index * slots_dev,
        lengths,
        state_pool,
        w_zxo,
        conv_x_pool,
        conv_bc_pool,
        table,
        jnp.concatenate([dt_bias, a_rate, skip_gain], axis=0),
    )

    mine = []
    own = []
    for tick in range(section_count):
        sent = project(
            parts,
            rounds,
            seq_dev,
            blocks,
            small_pad,
            place,
            gain_share,
            w,
            smalls,
            with_others(hidden),
        )
        made = mix(
            tick,
            parts,
            mp_count,
            model_width,
            place,
            past_x,
            past_bc,
            now_bc,
            wide,
            head,
            alive,
            held,
            to_heads(sent),
            mine,
        )
        mine = made[rounds:]
        kept, *others = finish(parts, group, place, w, to_blocks(made[:rounds]))
        total = kept.astype(jnp.float32)
        for r, other in enumerate(others):
            total = total + across(other, r + 1).astype(jnp.float32)
        total = total.astype(jnp.bfloat16)
        hidden, *own = settle(
            tick, group, blocks, chan_total, place, total, across(total, group), hidden, own
        )
        if tick + 1 < section_count:
            swaps = [
                pair
                for a in range(tick % 2, section_count - 1, 2)
                for pair in ((a, a + 1), (a + 1, a))
            ]
            hidden = lax.ppermute(hidden, "section", swaps)
    states = write_states(*mine, held)
    return (own[0][None], states)


def solution(mesh):
    placed = (
        P("dp", "mp"),
        P("dp"),
        P("dp"),
        P("section", None),
        P("section", None, "dp", "mp"),
        P("section", "dp", "mp"),
        P("section", None, "mp"),
        P("section", None, None),
        P("section", "dp", None, "mp"),
        P("section", "dp", None, None),
        P("section", "dp", "mp", None, None),
        P("section", "mp"),
        P("section", "mp"),
        P("section", "mp"),
        P("section", "mp"),
    )
    return jax.shard_map(
        local,
        mesh=mesh,
        in_specs=placed,
        out_specs=(P("section", "dp", "mp"), P("section", "dp", "mp", None, None)),
        check_vma=False,
    )
```

time: 994 us -> 216 us (0.22); the launches traced: 982 us -> 215 us
  waiting for transfers between devices: 336 us -> 71 us
  blocking collectives: 193 us -> 0 us
  matrix products: 161 us -> 0 us
  local copies, waits for them, and re-layouts: 129 us -> 6.32 us
  Pallas kernels: 0 us -> 63.4 us
  other arithmetic: 65.8 us -> 3.09 us
  between operations: 16.3 us -> 0.91 us
  starting transfers between devices: 80.8 us -> 70.6 us
    unnamed x21 -> x0, waiting for transfers between devices: 178 us -> none
    dot_general x28 -> x0, matrix products: 161 us -> none  [the longest x7 101 us: local(): jnp.einsum('bhpn,bn->bhp', new_state, conv_c, precision=lax.Precision.HIG...]
    psum x7 -> x0, waiting for transfers between devices: 130 us -> none  [local(): lax.psum(zx_part.astype(jnp.bfloat16), 'mp').astype(jnp.float32)]
    all_gather x21 -> x0, blocking collectives: 100 us -> none  [the longest x7 36.4 us: local(): rows_all = lax.all_gather(normed_share, 'dp', axis=0, tiled=True)]
    gather x21 -> x0, local copies, waits for them, and re-layouts: 84.9 us -> none  [the longest x7 76.5 us: local(): jnp.take(state_pool[0], rows_slot, axis=0) * alive[:, None, None, None]]
    psum x14 -> x0, blocking collectives: 73.5 us -> none  [the longest x7 38.8 us: local(): lax.psum(small_part.astype(jnp.bfloat16), 'mp').astype(jnp.float32)]
    ppermute x6 -> x49, waiting for transfers between devices: 0.02 us -> 71 us  [the longest x16 30.2 us: to_heads(): lax.ppermute(piece, ('dp', 'mp'), forward_pairs(r))]
    pallas_call x0 -> x18, Pallas kernels: none -> 63.4 us  [the longest x4 25.6 us: mix(): pl.pallas_call(functools.partial(mix_kernel, tick, rounds, parts, mp_coun...]
  transfers between devices with their start and end apart: 38 -> 49, of which waited for: 22 -> 29; matrix products, arithmetic and copies ran while one was open for 20% -> 1% of each run, Pallas kernels for 0% -> 8%
where the time goes in v1:
time: 216 us; the launch traced here: 215 us
  waiting for transfers between devices  71 us (33%)
  starting transfers between devices  70.6 us (33%)
  Pallas kernels  63.4 us (29%)
  local copies, waits for them, and re-layouts  6.32 us (3%)
  other arithmetic  3.09 us (1%)
    ppermute x16, waiting for transfers between devices, to_heads(): lax.ppermute(piece, ('dp', 'mp'), forward_pairs(r))  30.2 us
    pallas_call x4, Pallas kernels, mix(): pl.pallas_call(functools.partial(mix_kernel, tick, rounds, parts, mp_coun...  25.6 us
    ppermute x16, starting transfers between devices, to_blocks(): lax.ppermute(piece, ('dp', 'mp'), [(b, a) for a, b in forward_pairs(r)])  25.6 us
    ppermute x16, starting transfers between devices, to_heads(): lax.ppermute(piece, ('dp', 'mp'), forward_pairs(r))  24.2 us
    ppermute x14, waiting for transfers between devices, across(): return lax.ppermute(array, 'dp', [(d, d ^ by) for d in range(dp_count)])  22.7 us
    ppermute x16, waiting for transfers between devices, to_blocks(): lax.ppermute(piece, ('dp', 'mp'), [(b, a) for a, b in forward_pairs(r)])  12.7 us
    pallas_call x4, Pallas kernels, project(): pl.pallas_call(functools.partial(project_kernel, parts, seq_dev, len(smal...  11.8 us
    ppermute x14, starting transfers between devices, across(): return lax.ppermute(array, 'dp', [(d, d ^ by) for d in range(dp_count)])  11.2 us
  transfers between devices with their start and end apart: 49, of which 29 were waited for; matrix products, arithmetic and copies ran while one was open for 1% of the time, Pallas kernels for 8%

profile of v1, /device:TPU:0, one launch (start us, length us, event | category | flops | bytes accessed | tf_op | source)
XLA Modules:
  0.0 215.3 jit_solution(15605740067314136603)
XLA Ops:
  0.6 3.1 %collective-permute-start = (bf16[84,1280]{1,0:T(8,128)(2,1)}, bf16[84,1280]{1,0:T(8,128)(2,1)S(1)}, u32[]{:S(2)}, u32[]{:S(2)}) collective-permute-start(bf16[84,1280]{1,0:T(8,128)(2,1)} %bitcast.10), channel_id=1, source_target_pairs={{0,16},{8,24},{16,0},{24,8},{1,17},{9,25},{17,1},{25,9},{2,18},{10... | collective-permute-start | bytes 645128 | tf_op jit(solution)/shard_map/ppermute | solution.py:631
  3.8 0.8 fusion.table_ref
  5.4 4.9 %collective-permute-done.1 = bf16[16,1280]{1,0:T(8,128)(2,1)S(1)} collective-permute-done((bf16[16,1280]{1,0:T(8,128)(2,1)}, bf16[16,1280]{1,0:T(8,128)(2,1)S(1)}, u32[]{:S(2)}, u32[]{:S(2)}) %collective-permute-start.1) | collective-permute-done | bytes 40992 | tf_op jit(solution)/shard_map/ppermute | solution.py:631
  10.3 0.8 broadcast_select_fusion.1
  11.9 3.8 %copy-done.3 = bf16[1,3,1280,1280]{3,2,1,0:T(8,128)(2,1)S(1)} copy-done((bf16[1,3,1280,1280]{3,2,1,0:T(8,128)(2,1)S(1)}, bf16[1,3,1280,1280]{3,2,1,0:T(8,128)(2,1)}, u32[]{:S(2)}) %copy-start.3) | copy-done | bytes 9830424
  15.7 1.0 copy-done.5
  18.1 9.2 %load.1 = (f32[4,40,64,128]{3,2,1,0:T(8,128)S(1)}, f32[4,40,64,128]{3,2,1,0:T(8,128)S(1)}, f32[4,40,64,128]{3,2,1,0:T(8,128)S(1)}, f32[4,40,64,128]{3,2,1,0:T(8,...) custom-call(s32[16]{0:T(128)S(1)} %broadcast_subtract_fusion.slots_r, ...), custom_call_target="tpu_custom_call" | custom-call | flops 83886080 | bytes 30801920 | tf_op jit(solution)/shard_map/load/pallas_call | solution.py:163
  27.4 2.9 %project.4 = (bf16[16,3072]{1,0:T(8,128)(2,1)S(1)}, bf16[16,3072]{1,0:T(8,128)(2,1)S(1)}, bf16[16,3072]{1,0:T(8,128)(2,1)S(1)}, bf16[16,3072]{1,0:T(8,128)(2,1)S(1)}) custom-call(s32[5]{0:T(128)S(1)} %stack.20.place_ref, f32[1,1280]{1,0:T(1,128)S(1)} %constant_dynamic-slice_fusion.gain_ref, bf16[3,1280,1280]{2,1,0:T(8,128)(2,1)S(1)} %get-tuple-element.72.w_ref, ...), custom_call_target="tpu_custom_call" | custom-call | flops 482344960 | bytes 7536640 | tf_op jit(solution)/shard_map/project/pallas_call | solution.py:251
  31.6 5.3 %collective-permute-start.5 = (bf16[16,3072]{1,0:T(8,128)(2,1)S(1)}, bf16[16,3072]{1,0:T(8,128)(2,1)S(1)}, u32[]{:S(2)}, u32[]{:S(2)}) collective-permute-start(bf16[16,3072]{1,0:T(8,128)(2,1)S(1)} %get-tuple-element.85), channel_id=1, source_target_pairs={{0,16},{4,0},{8,24},{12,8},{16,20},{20,4},{24,28},{28,12},{1,17},{... | collective-permute-start | bytes 294920 | tf_op jit(solution)/shard_map/ppermute | solution.py:618
  36.9 6.4 %collective-permute-done.5.refs_6_ = bf16[16,3072]{1,0:T(8,128)(2,1)S(1)} collective-permute-done((bf16[16,3072]{1,0:T(8,128)(2,1)S(1)}, bf16[16,3072]{1,0:T(8,128)(2,1)S(1)}, u32[]{:S(2)}, u32[]{:S(2)}) %collective-permute-start.5) | collective-permute-done | bytes 98336 | tf_op jit(solution)/shard_map/ppermute | solution.py:618
  43.3 1.3 collective-permute-done.6.refs_7_
  44.6 6.4 %mix.4 = (bf16[16,1408]{1,0:T(8,128)(2,1)S(1)}, bf16[16,1408]{1,0:T(8,128)(2,1)S(1)}, bf16[16,1408]{1,0:T(8,128)(2,1)S(1)}, bf16[16,1408]{1,0:T(8,128)(2,1)S(1)}...) custom-call(s32[5]{0:T(128)S(1)} %stack.20.place_ref, ...), custom_call_target="tpu_custom_call" | custom-call | flops 83886080 | bytes 20971520 | tf_op jit(solution)/shard_map/mix/pallas_call | solution.py:394
  52.0 5.0 %collective-permute-start.9 = (bf16[16,1408]{1,0:T(8,128)(2,1)S(1)}, bf16[16,1408]{1,0:T(8,128)(2,1)S(1)}, u32[]{:S(2)}, u32[]{:S(2)}) collective-permute-start(bf16[16,1408]{1,0:T(8,128)(2,1)S(1)} %get-tuple-element.89), channel_id=1, source_target_pairs={{16,0},{0,4},{24,8},{8,12},{20,16},{4,20},{28,24},{12,28},{17,1},{... | collective-permute-start | bytes 135176 | tf_op jit(solution)/shard_map/ppermute | solution.py:623
  57.3 2.3 %collective-permute-done.9.refs_2_ = bf16[16,1408]{1,0:T(8,128)(2,1)S(1)} collective-permute-done((bf16[16,1408]{1,0:T(8,128)(2,1)S(1)}, bf16[16,1408]{1,0:T(8,128)(2,1)S(1)}, u32[]{:S(2)}, u32[]{:S(2)}) %collective-permute-start.9) | collective-permute-done | bytes 45088 | tf_op jit(solution)/shard_map/ppermute | solution.py:623
  59.6 0.9 collective-permute-done.10.refs_3_
  60.5 1.2 finish.4
  62.2 0.9 collective-permute-done.11
  63.1 1.5 collective-permute-start.12
  64.7 3.4 %collective-permute-done.12.met_ref = bf16[32,1408]{1,0:T(8,128)(2,1)S(1)} collective-permute-done((bf16[32,1408]{1,0:T(8,128)(2,1)S(1)}, bf16[32,1408]{1,0:T(8,128)(2,1)S(1)}, u32[]{:S(2)}, u32[]{:S(2)}) %collective-permute-start.12) | collective-permute-done | bytes 90144 | tf_op jit(solution)/shard_map/ppermute | solution.py:631
  68.7 1.6 collective-permute-start.13
  70.4 2.9 %collective-permute-done.13.refs_2_.old_ref = bf16[32,1280]{1,0:T(8,128)(2,1)S(1)} collective-permute-done((bf16[32,1280]{1,0:T(8,128)(2,1)S(1)}, bf16[32,1280]{1,0:T(8,128)(2,1)S(1)}, u32[]{:S(2)}, u32[]{:S(2)}) %collective-permute-start.13) | collective-permute-done | bytes 81952 | tf_op jit(solution)/shard_map/ppermute | solution.py:712
  73.2 1.3 collective-permute-done.14.refs_3_
  74.5 2.9 %project.5 = (bf16[16,3072]{1,0:T(8,128)(2,1)S(1)}, bf16[16,3072]{1,0:T(8,128)(2,1)S(1)}, bf16[16,3072]{1,0:T(8,128)(2,1)S(1)}, bf16[16,3072]{1,0:T(8,128)(2,1)S(1)}) custom-call(s32[5]{0:T(128)S(1)} %stack.20.place_ref, f32[1,1280]{1,0:T(1,128)S(1)} %constant_dynamic-slice_fusion.gain_ref, bf16[3,1280,1280]{2,1,0:T(8,128)(2,1)S(1)} %get-tuple-element.72.w_ref, ...), custom_call_target="tpu_custom_call" | custom-call | flops 482344960 | bytes 7536640 | tf_op jit(solution)/shard_map/project/pallas_call | solution.py:251
  78.4 4.8 %collective-permute-start.17 = (bf16[16,3072]{1,0:T(8,128)(2,1)S(1)}, bf16[16,3072]{1,0:T(8,128)(2,1)S(1)}, u32[]{:S(2)}, u32[]{:S(2)}) collective-permute-start(bf16[16,3072]{1,0:T(8,128)(2,1)S(1)} %get-tuple-element.96), channel_id=1, source_target_pairs={{0,16},{4,0},{8,24},{12,8},{16,20},{20,4},{24,28},{28,12},{1,17},{... | collective-permute-start | bytes 294920 | tf_op jit(solution)/shard_map/ppermute | solution.py:618
  83.4 6.2 %collective-permute-done.17.refs_6_ = bf16[16,3072]{1,0:T(8,128)(2,1)S(1)} collective-permute-done((bf16[16,3072]{1,0:T(8,128)(2,1)S(1)}, bf16[16,3072]{1,0:T(8,128)(2,1)S(1)}, u32[]{:S(2)}, u32[]{:S(2)}) %collective-permute-start.17) | collective-permute-done | bytes 98336 | tf_op jit(solution)/shard_map/ppermute | solution.py:618
  89.6 1.3 collective-permute-done.18.refs_7_
  90.9 6.4 %mix.5 = (bf16[16,1408]{1,0:T(8,128)(2,1)S(1)}, bf16[16,1408]{1,0:T(8,128)(2,1)S(1)}, bf16[16,1408]{1,0:T(8,128)(2,1)S(1)}, bf16[16,1408]{1,0:T(8,128)(2,1)S(1)}...) custom-call(s32[5]{0:T(128)S(1)} %stack.20.place_ref, ...), custom_call_target="tpu_custom_call" | custom-call | flops 83886080 | bytes 20971520 | tf_op jit(solution)/shard_map/mix/pallas_call | solution.py:394
  98.3 5.1 %collective-permute-start.21 = (bf16[16,1408]{1,0:T(8,128)(2,1)S(1)}, bf16[16,1408]{1,0:T(8,128)(2,1)S(1)}, u32[]{:S(2)}, u32[]{:S(2)}) collective-permute-start(bf16[16,1408]{1,0:T(8,128)(2,1)S(1)} %get-tuple-element.103), channel_id=1, source_target_pairs={{16,0},{0,4},{24,8},{8,12},{20,16},{4,20},{28,24},{12,28},{17,1},{... | collective-permute-start | bytes 135176 | tf_op jit(solution)/shard_map/ppermute | solution.py:623
  103.7 2.3 %collective-permute-done.21.refs_2_ = bf16[16,1408]{1,0:T(8,128)(2,1)S(1)} collective-permute-done((bf16[16,1408]{1,0:T(8,128)(2,1)S(1)}, bf16[16,1408]{1,0:T(8,128)(2,1)S(1)}, u32[]{:S(2)}, u32[]{:S(2)}) %collective-permute-start.21) | collective-permute-done | bytes 45088 | tf_op jit(solution)/shard_map/ppermute | solution.py:623
  105.9 0.9 collective-permute-done.22.refs_3_
  106.8 1.2 finish.5
  108.5 0.9 collective-permute-done.23
  109.5 1.5 collective-permute-start.24
  111.0 3.4 %collective-permute-done.24.met_ref = bf16[32,1408]{1,0:T(8,128)(2,1)S(1)} collective-permute-done((bf16[32,1408]{1,0:T(8,128)(2,1)S(1)}, bf16[32,1408]{1,0:T(8,128)(2,1)S(1)}, u32[]{:S(2)}, u32[]{:S(2)}) %collective-permute-start.24) | collective-permute-done | bytes 90144 | tf_op jit(solution)/shard_map/ppermute | solution.py:631
  115.9 1.3 collective-permute-done.26.refs_3_
  117.1 3.0 %project.6 = (bf16[16,3072]{1,0:T(8,128)(2,1)S(1)}, bf16[16,3072]{1,0:T(8,128)(2,1)S(1)}, bf16[16,3072]{1,0:T(8,128)(2,1)S(1)}, bf16[16,3072]{1,0:T(8,128)(2,1)S(1)}) custom-call(s32[5]{0:T(128)S(1)} %stack.20.place_ref, f32[1,1280]{1,0:T(1,128)S(1)} %constant_dynamic-slice_fusion.gain_ref, bf16[3,1280,1280]{2,1,0:T(8,128)(2,1)S(1)} %get-tuple-element.72.w_ref, ...), custom_call_target="tpu_custom_call" | custom-call | flops 482344960 | bytes 7536640 | tf_op jit(solution)/shard_map/project/pallas_call | solution.py:251
  121.0 4.8 %collective-permute-start.29 = (bf16[16,3072]{1,0:T(8,128)(2,1)S(1)}, bf16[16,3072]{1,0:T(8,128)(2,1)S(1)}, u32[]{:S(2)}, u32[]{:S(2)}) collective-permute-start(bf16[16,3072]{1,0:T(8,128)(2,1)S(1)} %get-tuple-element.111), channel_id=1, source_target_pairs={{0,16},{4,0},{8,24},{12,8},{16,20},{20,4},{24,28},{28,12},{1,17},{... | collective-permute-start | bytes 294920 | tf_op jit(solution)/shard_map/ppermute | solution.py:618
  126.0 6.2 %collective-permute-done.29.refs_6_ = bf16[16,3072]{1,0:T(8,128)(2,1)S(1)} collective-permute-done((bf16[16,3072]{1,0:T(8,128)(2,1)S(1)}, bf16[16,3072]{1,0:T(8,128)(2,1)S(1)}, u32[]{:S(2)}, u32[]{:S(2)}) %collective-permute-start.29) | collective-permute-done | bytes 98336 | tf_op jit(solution)/shard_map/ppermute | solution.py:618
  132.2 1.3 collective-permute-done.30.refs_7_
  133.5 6.4 %mix.6 = (bf16[16,1408]{1,0:T(8,128)(2,1)S(1)}, bf16[16,1408]{1,0:T(8,128)(2,1)S(1)}, bf16[16,1408]{1,0:T(8,128)(2,1)S(1)}, bf16[16,1408]{1,0:T(8,128)(2,1)S(1)}...) custom-call(s32[5]{0:T(128)S(1)} %stack.20.place_ref, ...), custom_call_target="tpu_custom_call" | custom-call | flops 83886080 | bytes 20971520 | tf_op jit(solution)/shard_map/mix/pallas_call | solution.py:394
  140.8 5.1 %collective-permute-start.33 = (bf16[16,1408]{1,0:T(8,128)(2,1)S(1)}, bf16[16,1408]{1,0:T(8,128)(2,1)S(1)}, u32[]{:S(2)}, u32[]{:S(2)}) collective-permute-start(bf16[16,1408]{1,0:T(8,128)(2,1)S(1)} %get-tuple-element.118), channel_id=1, source_target_pairs={{16,0},{0,4},{24,8},{8,12},{20,16},{4,20},{28,24},{12,28},{17,1},{... | collective-permute-start | bytes 135176 | tf_op jit(solution)/shard_map/ppermute | solution.py:623
  146.2 2.3 %collective-permute-done.33.refs_2_ = bf16[16,1408]{1,0:T(8,128)(2,1)S(1)} collective-permute-done((bf16[16,1408]{1,0:T(8,128)(2,1)S(1)}, bf16[16,1408]{1,0:T(8,128)(2,1)S(1)}, u32[]{:S(2)}, u32[]{:S(2)}) %collective-permute-start.33) | collective-permute-done | bytes 45088 | tf_op jit(solution)/shard_map/ppermute | solution.py:623
  148.5 0.9 collective-permute-done.34.refs_3_
  149.4 1.2 finish.6
  151.1 0.9 collective-permute-done.35
  152.1 1.5 collective-permute-start.36
  153.6 3.4 %collective-permute-done.36.met_ref = bf16[32,1408]{1,0:T(8,128)(2,1)S(1)} collective-permute-done((bf16[32,1408]{1,0:T(8,128)(2,1)S(1)}, bf16[32,1408]{1,0:T(8,128)(2,1)S(1)}, u32[]{:S(2)}, u32[]{:S(2)}) %collective-permute-start.36) | collective-permute-done | bytes 90144 | tf_op jit(solution)/shard_map/ppermute | solution.py:631
  157.7 7.2 %collective-permute-start.37 = (bf16[32,1280]{1,0:T(8,128)(2,1)S(1)}, bf16[32,1280]{1,0:T(8,128)(2,1)S(1)}, u32[]{:S(2)}, u32[]{:S(2)}) collective-permute-start(bf16[32,1280]{1,0:T(8,128)(2,1)S(1)} %get-tuple-element.123), channel_id=1, source_target_pairs={{0,1},{1,0},{2,3},{3,2},{4,5},{5,4},{6,7},{7,6},{8,9},{9,8},{10,11... | collective-permute-start | bytes 245768 | tf_op jit(solution)/shard_map/ppermute | solution.py:712
  164.9 2.4 %collective-permute-done.37.refs_2_.old_ref = bf16[32,1280]{1,0:T(8,128)(2,1)S(1)} collective-permute-done((bf16[32,1280]{1,0:T(8,128)(2,1)S(1)}, bf16[32,1280]{1,0:T(8,128)(2,1)S(1)}, u32[]{:S(2)}, u32[]{:S(2)}) %collective-permute-start.37) | collective-permute-done | bytes 81952 | tf_op jit(solution)/shard_map/ppermute | solution.py:712
  167.3 1.3 collective-permute-done.38.refs_3_
  168.6 2.9 %project.7 = (bf16[16,3072]{1,0:T(8,128)(2,1)S(1)}, bf16[16,3072]{1,0:T(8,128)(2,1)S(1)}, bf16[16,3072]{1,0:T(8,128)(2,1)S(1)}, bf16[16,3072]{1,0:T(8,128)(2,1)S(1)}) custom-call(s32[5]{0:T(128)S(1)} %stack.20.place_ref, f32[1,1280]{1,0:T(1,128)S(1)} %constant_dynamic-slice_fusion.gain_ref, bf16[3,1280,1280]{2,1,0:T(8,128)(2,1)S(1)} %get-tuple-element.72.w_ref, ...), custom_call_target="tpu_custom_call" | custom-call | flops 482344960 | bytes 7536640 | tf_op jit(solution)/shard_map/project/pallas_call | solution.py:251
  172.5 4.8 %collective-permute-start.41 = (bf16[16,3072]{1,0:T(8,128)(2,1)S(1)}, bf16[16,3072]{1,0:T(8,128)(2,1)S(1)}, u32[]{:S(2)}, u32[]{:S(2)}) collective-permute-start(bf16[16,3072]{1,0:T(8,128)(2,1)S(1)} %get-tuple-element.126), channel_id=1, source_target_pairs={{0,16},{4,0},{8,24},{12,8},{16,20},{20,4},{24,28},{28,12},{1,17},{... | collective-permute-start | bytes 294920 | tf_op jit(solution)/shard_map/ppermute | solution.py:618
  177.5 6.2 %collective-permute-done.41.refs_6_ = bf16[16,3072]{1,0:T(8,128)(2,1)S(1)} collective-permute-done((bf16[16,3072]{1,0:T(8,128)(2,1)S(1)}, bf16[16,3072]{1,0:T(8,128)(2,1)S(1)}, u32[]{:S(2)}, u32[]{:S(2)}) %collective-permute-start.41) | collective-permute-done | bytes 98336 | tf_op jit(solution)/shard_map/ppermute | solution.py:618
  183.7 1.3 collective-permute-done.42.refs_7_
  185.0 6.4 %mix.7 = (bf16[16,1408]{1,0:T(8,128)(2,1)S(1)}, bf16[16,1408]{1,0:T(8,128)(2,1)S(1)}, bf16[16,1408]{1,0:T(8,128)(2,1)S(1)}, bf16[16,1408]{1,0:T(8,128)(2,1)S(1)}...) custom-call(s32[5]{0:T(128)S(1)} %stack.20.place_ref, ...), custom_call_target="tpu_custom_call" | custom-call | flops 83886080 | bytes 20971520 | tf_op jit(solution)/shard_map/mix/pallas_call | solution.py:394
  191.4 0.8 collective-permute-start.43
  192.5 5.2 %collective-permute-start.45 = (bf16[16,1408]{1,0:T(8,128)(2,1)S(1)}, bf16[16,1408]{1,0:T(8,128)(2,1)S(1)}, u32[]{:S(2)}, u32[]{:S(2)}) collective-permute-start(bf16[16,1408]{1,0:T(8,128)(2,1)S(1)} %get-tuple-element.133), channel_id=1, source_target_pairs={{16,0},{0,4},{24,8},{8,12},{20,16},{4,20},{28,24},{12,28},{17,1},{... | collective-permute-start | bytes 135176 | tf_op jit(solution)/shard_map/ppermute | solution.py:623
  198.0 2.3 %collective-permute-done.45.refs_2_ = bf16[16,1408]{1,0:T(8,128)(2,1)S(1)} collective-permute-done((bf16[16,1408]{1,0:T(8,128)(2,1)S(1)}, bf16[16,1408]{1,0:T(8,128)(2,1)S(1)}, u32[]{:S(2)}, u32[]{:S(2)}) %collective-permute-start.45) | collective-permute-done | bytes 45088 | tf_op jit(solution)/shard_map/ppermute | solution.py:623
  200.3 0.9 collective-permute-done.46.refs_3_
  201.2 1.2 finish.7
  202.9 0.9 collective-permute-done.47
  203.8 1.5 collective-permute-start.48
  205.4 8.6 %write_states.1 = f32[1,16,40,64,128]{4,3,2,1,0:T(8,128)} custom-call(f32[16,40]{1,0:T(8,128)S(1)} %get-tuple-element.139.decay_ref, f32[16,2560]{1,0:T(8,128)S(1)} %get-tuple-element.140.x_ref, f32[16,128]{1,0:T(8,128)S(1)} %get-tuple-element.141.b_ref, f32[4,40,64,128]{3,2,1,0:T(8,128)S(1)} %get-tuple-element.79.refs_0_, ...), custom_call_target="tpu_custom_call" | custom-call | flops 83886080 | bytes 41943040 | tf_op jit(solution)/shard_map/write_states/pallas_call | solution.py:540
  214.0 1.3 settle.7
  (84 shorter events, 16.6 us)
Async XLA Ops:
  0.6 3.2 %copy-start = (f32[1,2560]{1,0:T(1,128)S(1)}, f32[1,2560]{1,0:T(1,128)}, u32[]{:S(2)}) copy-start(f32[1,2560]{1,0:T(1,128)} %param.18) | copy-start | bytes 30724
  0.6 26.7 %collective-permute-start = (bf16[84,1280]{1,0:T(8,128)(2,1)}, bf16[84,1280]{1,0:T(8,128)(2,1)S(1)}, u32[]{:S(2)}, u32[]{:S(2)}) collective-permute-start(bf16[84,1280]{1,0:T(8,128)(2,1)} %bitcast.10), channel_id=1, source_target_pairs={{0,16},{8,24},{16,0},{24,8},{1,17},{9,25},{17,1},{25,9},{2,18},{10... | collective-permute-start | bytes 645128 | tf_op jit(solution)/shard_map/ppermute | solution.py:631
  3.7 6.6 %collective-permute-start.1 = (bf16[16,1280]{1,0:T(8,128)(2,1)}, bf16[16,1280]{1,0:T(8,128)(2,1)S(1)}, u32[]{:S(2)}, u32[]{:S(2)}) collective-permute-start(bf16[16,1280]{1,0:T(8,128)(2,1)} %param.15), channel_id=1, source_target_pairs={{0,16},{8,24},{16,0},{24,8},{1,17},{9,25},{17,1},{25,9},{2,18},{10... | collective-permute-start | bytes 122888 | tf_op jit(solution)/shard_map/ppermute | solution.py:631
  11.1 16.2 %collective-permute-start.2 = (bf16[32,1280]{1,0:T(8,128)(2,1)S(1)}, bf16[32,1280]{1,0:T(8,128)(2,1)S(1)}, u32[]{:S(2)}, u32[]{:S(2)}) collective-permute-start(bf16[32,1280]{1,0:T(8,128)(2,1)S(1)} %pad_maximum_fusion.refs_2_.old_ref), channel_id=1, source_target_pairs={{0,8},{8,0},{16,24},{24,16},{1,9},{9,1},{17,25},{25,17},{2,10},{10... | collective-permute-start | bytes 245768 | tf_op jit(solution)/shard_map/ppermute | solution.py:631
  11.9 3.8 %copy-start.3 = (bf16[1,3,1280,1280]{3,2,1,0:T(8,128)(2,1)S(1)}, bf16[1,3,1280,1280]{3,2,1,0:T(8,128)(2,1)}, u32[]{:S(2)}) copy-start(bf16[1,3,1280,1280]{3,2,1,0:T(8,128)(2,1)} %w_ref.1) | copy-start | bytes 29491204
  15.7 1.0 copy-start.5
  16.7 0.8 copy-start.6
  17.4 0.7 copy-start.7
  18.1 9.3 %copy-start.4 = (bf16[1,84,1280]{2,1,0:T(8,128)(2,1)S(1)}, bf16[1,84,1280]{2,1,0:T(8,128)(2,1)}, u32[]{:S(2)}) copy-start(bf16[1,84,1280]{2,1,0:T(8,128)(2,1)} %param.20) | copy-start | bytes 645124
  27.3 157.6 %copy-start.2 = (f32[4,40,64,128]{3,2,1,0:T(8,128)}, f32[4,40,64,128]{3,2,1,0:T(8,128)S(1)}, u32[]{:S(2)}) copy-start(f32[4,40,64,128]{3,2,1,0:T(8,128)S(1)} %get-tuple-element.82.refs_3_) | copy-start | bytes 15728644
  30.3 6.5 %collective-permute-start.3 = (bf16[16,3072]{1,0:T(8,128)(2,1)S(1)}, bf16[16,3072]{1,0:T(8,128)(2,1)S(1)}, u32[]{:S(2)}, u32[]{:S(2)}) collective-permute-start(bf16[16,3072]{1,0:T(8,128)(2,1)S(1)} %get-tuple-element.83), channel_id=1, source_target_pairs={{0,0},{4,16},{8,8},{12,24},{16,4},{20,20},{24,12},{28,28},{1,1},{5... | collective-permute-start | bytes 294920 | tf_op jit(solution)/shard_map/ppermute | solution.py:618
  31.0 5.9 %collective-permute-start.4 = (bf16[16,3072]{1,0:T(8,128)(2,1)S(1)}, bf16[16,3072]{1,0:T(8,128)(2,1)S(1)}, u32[]{:S(2)}, u32[]{:S(2)}) collective-permute-start(bf16[16,3072]{1,0:T(8,128)(2,1)S(1)} %get-tuple-element.84), channel_id=1, source_target_pairs={{0,8},{4,24},{8,0},{12,16},{16,12},{20,28},{24,4},{28,20},{1,9},{5... | collective-permute-start | bytes 294920 | tf_op jit(solution)/shard_map/ppermute | solution.py:618
  31.6 11.8 %collective-permute-start.5 = (bf16[16,3072]{1,0:T(8,128)(2,1)S(1)}, bf16[16,3072]{1,0:T(8,128)(2,1)S(1)}, u32[]{:S(2)}, u32[]{:S(2)}) collective-permute-start(bf16[16,3072]{1,0:T(8,128)(2,1)S(1)} %get-tuple-element.85), channel_id=1, source_target_pairs={{0,16},{4,0},{8,24},{12,8},{16,20},{20,4},{24,28},{28,12},{1,17},{... | collective-permute-start | bytes 294920 | tf_op jit(solution)/shard_map/ppermute | solution.py:618
  36.9 7.8 %collective-permute-start.6 = (bf16[16,3072]{1,0:T(8,128)(2,1)S(1)}, bf16[16,3072]{1,0:T(8,128)(2,1)S(1)}, u32[]{:S(2)}, u32[]{:S(2)}) collective-permute-start(bf16[16,3072]{1,0:T(8,128)(2,1)S(1)} %get-tuple-element.86), channel_id=1, source_target_pairs={{0,24},{4,8},{8,16},{12,0},{16,28},{20,12},{24,20},{28,4},{1,25},{... | collective-permute-start | bytes 294920 | tf_op jit(solution)/shard_map/ppermute | solution.py:618
  51.0 6.3 %collective-permute-start.7 = (bf16[16,1408]{1,0:T(8,128)(2,1)S(1)}, bf16[16,1408]{1,0:T(8,128)(2,1)S(1)}, u32[]{:S(2)}, u32[]{:S(2)}) collective-permute-start(bf16[16,1408]{1,0:T(8,128)(2,1)S(1)} %get-tuple-element.87), channel_id=1, source_target_pairs={{0,0},{16,4},{8,8},{24,12},{4,16},{20,20},{12,24},{28,28},{1,1},{1... | collective-permute-start | bytes 135176 | tf_op jit(solution)/shard_map/ppermute | solution.py:623
  51.7 5.6 %collective-permute-start.8 = (bf16[16,1408]{1,0:T(8,128)(2,1)S(1)}, bf16[16,1408]{1,0:T(8,128)(2,1)S(1)}, u32[]{:S(2)}, u32[]{:S(2)}) collective-permute-start(bf16[16,1408]{1,0:T(8,128)(2,1)S(1)} %get-tuple-element.88), channel_id=1, source_target_pairs={{8,0},{24,4},{0,8},{16,12},{12,16},{28,20},{4,24},{20,28},{9,1},{2... | collective-permute-start | bytes 135176 | tf_op jit(solution)/shard_map/ppermute | solution.py:623
  52.0 7.6 %collective-permute-start.9 = (bf16[16,1408]{1,0:T(8,128)(2,1)S(1)}, bf16[16,1408]{1,0:T(8,128)(2,1)S(1)}, u32[]{:S(2)}, u32[]{:S(2)}) collective-permute-start(bf16[16,1408]{1,0:T(8,128)(2,1)S(1)} %get-tuple-element.89), channel_id=1, source_target_pairs={{16,0},{0,4},{24,8},{8,12},{20,16},{4,20},{28,24},{12,28},{17,1},{... | collective-permute-start | bytes 135176 | tf_op jit(solution)/shard_map/ppermute | solution.py:623
  57.0 3.5 %collective-permute-start.10 = (bf16[16,1408]{1,0:T(8,128)(2,1)S(1)}, bf16[16,1408]{1,0:T(8,128)(2,1)S(1)}, u32[]{:S(2)}, u32[]{:S(2)}) collective-permute-start(bf16[16,1408]{1,0:T(8,128)(2,1)S(1)} %get-tuple-element.90), channel_id=1, source_target_pairs={{24,0},{8,4},{16,8},{0,12},{28,16},{12,20},{20,24},{4,28},{25,1},{... | collective-permute-start | bytes 135176 | tf_op jit(solution)/shard_map/ppermute | solution.py:623
  61.7 1.4 collective-permute-start.11
  63.1 4.9 %collective-permute-start.12 = (bf16[32,1408]{1,0:T(8,128)(2,1)S(1)}, bf16[32,1408]{1,0:T(8,128)(2,1)S(1)}, u32[]{:S(2)}, u32[]{:S(2)}) collective-permute-start(bf16[32,1408]{1,0:T(8,128)(2,1)S(1)} %add_convert_fusion.3.mine_ref), channel_id=1, source_target_pairs={{0,16},{8,24},{16,0},{24,8},{1,17},{9,25},{17,1},{25,9},{2,18},{10... | collective-permute-start | bytes 270344 | tf_op jit(solution)/shard_map/ppermute | solution.py:631
  68.7 4.5 %collective-permute-start.13 = (bf16[32,1280]{1,0:T(8,128)(2,1)S(1)}, bf16[32,1280]{1,0:T(8,128)(2,1)S(1)}, u32[]{:S(2)}, u32[]{:S(2)}) collective-permute-start(bf16[32,1280]{1,0:T(8,128)(2,1)S(1)} %get-tuple-element.93), channel_id=1, source_target_pairs={{0,1},{1,0},{2,3},{3,2},{4,5},{5,4},{6,7},{7,6},{8,9},{9,8},{10,11... | collective-permute-start | bytes 245768 | tf_op jit(solution)/shard_map/ppermute | solution.py:712
  73.2 1.3 collective-permute-start.14
  77.5 5.9 %collective-permute-start.15 = (bf16[16,3072]{1,0:T(8,128)(2,1)S(1)}, bf16[16,3072]{1,0:T(8,128)(2,1)S(1)}, u32[]{:S(2)}, u32[]{:S(2)}) collective-permute-start(bf16[16,3072]{1,0:T(8,128)(2,1)S(1)} %get-tuple-element.94), channel_id=1, source_target_pairs={{0,0},{4,16},{8,8},{12,24},{16,4},{20,20},{24,12},{28,28},{1,1},{5... | collective-permute-start | bytes 294920 | tf_op jit(solution)/shard_map/ppermute | solution.py:618
  78.2 5.2 %collective-permute-start.16 = (bf16[16,3072]{1,0:T(8,128)(2,1)S(1)}, bf16[16,3072]{1,0:T(8,128)(2,1)S(1)}, u32[]{:S(2)}, u32[]{:S(2)}) collective-permute-start(bf16[16,3072]{1,0:T(8,128)(2,1)S(1)} %get-tuple-element.95), channel_id=1, source_target_pairs={{0,8},{4,24},{8,0},{12,16},{16,12},{20,28},{24,4},{28,20},{1,9},{5... | collective-permute-start | bytes 294920 | tf_op jit(solution)/shard_map/ppermute | solution.py:618
  78.4 11.2 %collective-permute-start.17 = (bf16[16,3072]{1,0:T(8,128)(2,1)S(1)}, bf16[16,3072]{1,0:T(8,128)(2,1)S(1)}, u32[]{:S(2)}, u32[]{:S(2)}) collective-permute-start(bf16[16,3072]{1,0:T(8,128)(2,1)S(1)} %get-tuple-element.96), channel_id=1, source_target_pairs={{0,16},{4,0},{8,24},{12,8},{16,20},{20,4},{24,28},{28,12},{1,17},{... | collective-permute-start | bytes 294920 | tf_op jit(solution)/shard_map/ppermute | solution.py:618
  83.2 7.7 %collective-permute-start.18 = (bf16[16,3072]{1,0:T(8,128)(2,1)S(1)}, bf16[16,3072]{1,0:T(8,128)(2,1)S(1)}, u32[]{:S(2)}, u32[]{:S(2)}) collective-permute-start(bf16[16,3072]{1,0:T(8,128)(2,1)S(1)} %get-tuple-element.97), channel_id=1, source_target_pairs={{0,24},{4,8},{8,16},{12,0},{16,28},{20,12},{24,20},{28,4},{1,25},{... | collective-permute-start | bytes 294920 | tf_op jit(solution)/shard_map/ppermute | solution.py:618
  97.3 6.4 %collective-permute-start.19 = (bf16[16,1408]{1,0:T(8,128)(2,1)S(1)}, bf16[16,1408]{1,0:T(8,128)(2,1)S(1)}, u32[]{:S(2)}, u32[]{:S(2)}) collective-permute-start(bf16[16,1408]{1,0:T(8,128)(2,1)S(1)} %get-tuple-element.101), channel_id=1, source_target_pairs={{0,0},{16,4},{8,8},{24,12},{4,16},{20,20},{12,24},{28,28},{1,1},{1... | collective-permute-start | bytes 135176 | tf_op jit(solution)/shard_map/ppermute | solution.py:623
  98.0 5.7 %collective-permute-start.20 = (bf16[16,1408]{1,0:T(8,128)(2,1)S(1)}, bf16[16,1408]{1,0:T(8,128)(2,1)S(1)}, u32[]{:S(2)}, u32[]{:S(2)}) collective-permute-start(bf16[16,1408]{1,0:T(8,128)(2,1)S(1)} %get-tuple-element.102), channel_id=1, source_target_pairs={{8,0},{24,4},{0,8},{16,12},{12,16},{28,20},{4,24},{20,28},{9,1},{2... | collective-permute-start | bytes 135176 | tf_op jit(solution)/shard_map/ppermute | solution.py:623
  98.3 7.7 %collective-permute-start.21 = (bf16[16,1408]{1,0:T(8,128)(2,1)S(1)}, bf16[16,1408]{1,0:T(8,128)(2,1)S(1)}, u32[]{:S(2)}, u32[]{:S(2)}) collective-permute-start(bf16[16,1408]{1,0:T(8,128)(2,1)S(1)} %get-tuple-element.103), channel_id=1, source_target_pairs={{16,0},{0,4},{24,8},{8,12},{20,16},{4,20},{28,24},{12,28},{17,1},{... | collective-permute-start | bytes 135176 | tf_op jit(solution)/shard_map/ppermute | solution.py:623
  103.4 3.5 %collective-permute-start.22 = (bf16[16,1408]{1,0:T(8,128)(2,1)S(1)}, bf16[16,1408]{1,0:T(8,128)(2,1)S(1)}, u32[]{:S(2)}, u32[]{:S(2)}) collective-permute-start(bf16[16,1408]{1,0:T(8,128)(2,1)S(1)} %get-tuple-element.104), channel_id=1, source_target_pairs={{24,0},{8,4},{16,8},{0,12},{28,16},{12,20},{20,24},{4,28},{25,1},{... | collective-permute-start | bytes 135176 | tf_op jit(solution)/shard_map/ppermute | solution.py:623
  108.1 1.4 collective-permute-start.23
  109.5 4.9 %collective-permute-start.24 = (bf16[32,1408]{1,0:T(8,128)(2,1)S(1)}, bf16[32,1408]{1,0:T(8,128)(2,1)S(1)}, u32[]{:S(2)}, u32[]{:S(2)}) collective-permute-start(bf16[32,1408]{1,0:T(8,128)(2,1)S(1)} %add_convert_fusion.2.mine_ref), channel_id=1, source_target_pairs={{0,16},{8,24},{16,0},{24,8},{1,17},{9,25},{17,1},{25,9},{2,18},{10... | collective-permute-start | bytes 270344 | tf_op jit(solution)/shard_map/ppermute | solution.py:631
  115.1 0.7 collective-permute-start.25
  115.8 1.3 collective-permute-start.26
  120.1 5.9 %collective-permute-start.27 = (bf16[16,3072]{1,0:T(8,128)(2,1)S(1)}, bf16[16,3072]{1,0:T(8,128)(2,1)S(1)}, u32[]{:S(2)}, u32[]{:S(2)}) collective-permute-start(bf16[16,3072]{1,0:T(8,128)(2,1)S(1)} %get-tuple-element.109), channel_id=1, source_target_pairs={{0,0},{4,16},{8,8},{12,24},{16,4},{20,20},{24,12},{28,28},{1,1},{5... | collective-permute-start | bytes 294920 | tf_op jit(solution)/shard_map/ppermute | solution.py:618
  120.8 5.2 %collective-permute-start.28 = (bf16[16,3072]{1,0:T(8,128)(2,1)S(1)}, bf16[16,3072]{1,0:T(8,128)(2,1)S(1)}, u32[]{:S(2)}, u32[]{:S(2)}) collective-permute-start(bf16[16,3072]{1,0:T(8,128)(2,1)S(1)} %get-tuple-element.110), channel_id=1, source_target_pairs={{0,8},{4,24},{8,0},{12,16},{16,12},{20,28},{24,4},{28,20},{1,9},{5... | collective-permute-start | bytes 294920 | tf_op jit(solution)/shard_map/ppermute | solution.py:618
  121.0 11.2 %collective-permute-start.29 = (bf16[16,3072]{1,0:T(8,128)(2,1)S(1)}, bf16[16,3072]{1,0:T(8,128)(2,1)S(1)}, u32[]{:S(2)}, u32[]{:S(2)}) collective-permute-start(bf16[16,3072]{1,0:T(8,128)(2,1)S(1)} %get-tuple-element.111), channel_id=1, source_target_pairs={{0,16},{4,0},{8,24},{12,8},{16,20},{20,4},{24,28},{28,12},{1,17},{... | collective-permute-start | bytes 294920 | tf_op jit(solution)/shard_map/ppermute | solution.py:618
  125.7 7.8 %collective-permute-start.30 = (bf16[16,3072]{1,0:T(8,128)(2,1)S(1)}, bf16[16,3072]{1,0:T(8,128)(2,1)S(1)}, u32[]{:S(2)}, u32[]{:S(2)}) collective-permute-start(bf16[16,3072]{1,0:T(8,128)(2,1)S(1)} %get-tuple-element.112), channel_id=1, source_target_pairs={{0,24},{4,8},{8,16},{12,0},{16,28},{20,12},{24,20},{28,4},{1,25},{... | collective-permute-start | bytes 294920 | tf_op jit(solution)/shard_map/ppermute | solution.py:618
  139.9 6.4 %collective-permute-start.31 = (bf16[16,1408]{1,0:T(8,128)(2,1)S(1)}, bf16[16,1408]{1,0:T(8,128)(2,1)S(1)}, u32[]{:S(2)}, u32[]{:S(2)}) collective-permute-start(bf16[16,1408]{1,0:T(8,128)(2,1)S(1)} %get-tuple-element.116), channel_id=1, source_target_pairs={{0,0},{16,4},{8,8},{24,12},{4,16},{20,20},{12,24},{28,28},{1,1},{1... | collective-permute-start | bytes 135176 | tf_op jit(solution)/shard_map/ppermute | solution.py:623
  140.6 5.7 %collective-permute-start.32 = (bf16[16,1408]{1,0:T(8,128)(2,1)S(1)}, bf16[16,1408]{1,0:T(8,128)(2,1)S(1)}, u32[]{:S(2)}, u32[]{:S(2)}) collective-permute-start(bf16[16,1408]{1,0:T(8,128)(2,1)S(1)} %get-tuple-element.117), channel_id=1, source_target_pairs={{8,0},{24,4},{0,8},{16,12},{12,16},{28,20},{4,24},{20,28},{9,1},{2... | collective-permute-start | bytes 135176 | tf_op jit(solution)/shard_map/ppermute | solution.py:623
  140.8 7.7 %collective-permute-start.33 = (bf16[16,1408]{1,0:T(8,128)(2,1)S(1)}, bf16[16,1408]{1,0:T(8,128)(2,1)S(1)}, u32[]{:S(2)}, u32[]{:S(2)}) collective-permute-start(bf16[16,1408]{1,0:T(8,128)(2,1)S(1)} %get-tuple-element.118), channel_id=1, source_target_pairs={{16,0},{0,4},{24,8},{8,12},{20,16},{4,20},{28,24},{12,28},{17,1},{... | collective-permute-start | bytes 135176 | tf_op jit(solution)/shard_map/ppermute | solution.py:623
  146.0 3.5 %collective-permute-start.34 = (bf16[16,1408]{1,0:T(8,128)(2,1)S(1)}, bf16[16,1408]{1,0:T(8,128)(2,1)S(1)}, u32[]{:S(2)}, u32[]{:S(2)}) collective-permute-start(bf16[16,1408]{1,0:T(8,128)(2,1)S(1)} %get-tuple-element.119), channel_id=1, source_target_pairs={{24,0},{8,4},{16,8},{0,12},{28,16},{12,20},{20,24},{4,28},{25,1},{... | collective-permute-start | bytes 135176 | tf_op jit(solution)/shard_map/ppermute | solution.py:623
  150.7 1.4 collective-permute-start.35
  152.1 4.9 %collective-permute-start.36 = (bf16[32,1408]{1,0:T(8,128)(2,1)S(1)}, bf16[32,1408]{1,0:T(8,128)(2,1)S(1)}, u32[]{:S(2)}, u32[]{:S(2)}) collective-permute-start(bf16[32,1408]{1,0:T(8,128)(2,1)S(1)} %add_convert_fusion.1.mine_ref), channel_id=1, source_target_pairs={{0,16},{8,24},{16,0},{24,8},{1,17},{9,25},{17,1},{25,9},{2,18},{10... | collective-permute-start | bytes 270344 | tf_op jit(solution)/shard_map/ppermute | solution.py:631
  157.7 9.6 %collective-permute-start.37 = (bf16[32,1280]{1,0:T(8,128)(2,1)S(1)}, bf16[32,1280]{1,0:T(8,128)(2,1)S(1)}, u32[]{:S(2)}, u32[]{:S(2)}) collective-permute-start(bf16[32,1280]{1,0:T(8,128)(2,1)S(1)} %get-tuple-element.123), channel_id=1, source_target_pairs={{0,1},{1,0},{2,3},{3,2},{4,5},{5,4},{6,7},{7,6},{8,9},{9,8},{10,11... | collective-permute-start | bytes 245768 | tf_op jit(solution)/shard_map/ppermute | solution.py:712
  167.3 1.3 collective-permute-start.38
  171.6 5.9 %collective-permute-start.39 = (bf16[16,3072]{1,0:T(8,128)(2,1)S(1)}, bf16[16,3072]{1,0:T(8,128)(2,1)S(1)}, u32[]{:S(2)}, u32[]{:S(2)}) collective-permute-start(bf16[16,3072]{1,0:T(8,128)(2,1)S(1)} %get-tuple-element.124), channel_id=1, source_target_pairs={{0,0},{4,16},{8,8},{12,24},{16,4},{20,20},{24,12},{28,28},{1,1},{5... | collective-permute-start | bytes 294920 | tf_op jit(solution)/shard_map/ppermute | solution.py:618
  172.2 5.2 %collective-permute-start.40 = (bf16[16,3072]{1,0:T(8,128)(2,1)S(1)}, bf16[16,3072]{1,0:T(8,128)(2,1)S(1)}, u32[]{:S(2)}, u32[]{:S(2)}) collective-permute-start(bf16[16,3072]{1,0:T(8,128)(2,1)S(1)} %get-tuple-element.125), channel_id=1, source_target_pairs={{0,8},{4,24},{8,0},{12,16},{16,12},{20,28},{24,4},{28,20},{1,9},{5... | collective-permute-start | bytes 294920 | tf_op jit(solution)/shard_map/ppermute | solution.py:618
  172.5 11.2 %collective-permute-start.41 = (bf16[16,3072]{1,0:T(8,128)(2,1)S(1)}, bf16[16,3072]{1,0:T(8,128)(2,1)S(1)}, u32[]{:S(2)}, u32[]{:S(2)}) collective-permute-start(bf16[16,3072]{1,0:T(8,128)(2,1)S(1)} %get-tuple-element.126), channel_id=1, source_target_pairs={{0,16},{4,0},{8,24},{12,8},{16,20},{20,4},{24,28},{28,12},{1,17},{... | collective-permute-start | bytes 294920 | tf_op jit(solution)/shard_map/ppermute | solution.py:618
  177.2 7.7 %collective-permute-start.42 = (bf16[16,3072]{1,0:T(8,128)(2,1)S(1)}, bf16[16,3072]{1,0:T(8,128)(2,1)S(1)}, u32[]{:S(2)}, u32[]{:S(2)}) collective-permute-start(bf16[16,3072]{1,0:T(8,128)(2,1)S(1)} %get-tuple-element.127), channel_id=1, source_target_pairs={{0,24},{4,8},{8,16},{12,0},{16,28},{20,12},{24,20},{28,4},{1,25},{... | collective-permute-start | bytes 294920 | tf_op jit(solution)/shard_map/ppermute | solution.py:618
  191.4 14.0 %slice-start = ((s8[5242880]{0:T(1024)(128)(4,1)}), s8[4194304]{0:T(1024)(128)(4,1)S(1)}, s32[]{:S(2)}) async-start(s8[5242880]{0:T(1024)(128)(4,1)} %bitcast.8), calls=%async_computation | async-start | bytes 8388608
  191.4 6.6 %collective-permute-start.43 = (bf16[16,1408]{1,0:T(8,128)(2,1)S(1)}, bf16[16,1408]{1,0:T(8,128)(2,1)S(1)}, u32[]{:S(2)}, u32[]{:S(2)}) collective-permute-start(bf16[16,1408]{1,0:T(8,128)(2,1)S(1)} %get-tuple-element.131), channel_id=1, source_target_pairs={{0,0},{16,4},{8,8},{24,12},{4,16},{20,20},{12,24},{28,28},{1,1},{1... | collective-permute-start | bytes 135176 | tf_op jit(solution)/shard_map/ppermute | solution.py:623
  192.2 5.8 %collective-permute-start.44 = (bf16[16,1408]{1,0:T(8,128)(2,1)S(1)}, bf16[16,1408]{1,0:T(8,128)(2,1)S(1)}, u32[]{:S(2)}, u32[]{:S(2)}) collective-permute-start(bf16[16,1408]{1,0:T(8,128)(2,1)S(1)} %get-tuple-element.132), channel_id=1, source_target_pairs={{8,0},{24,4},{0,8},{16,12},{12,16},{28,20},{4,24},{20,28},{9,1},{2... | collective-permute-start | bytes 135176 | tf_op jit(solution)/shard_map/ppermute | solution.py:623
  192.5 7.8 %collective-permute-start.45 = (bf16[16,1408]{1,0:T(8,128)(2,1)S(1)}, bf16[16,1408]{1,0:T(8,128)(2,1)S(1)}, u32[]{:S(2)}, u32[]{:S(2)}) collective-permute-start(bf16[16,1408]{1,0:T(8,128)(2,1)S(1)} %get-tuple-element.133), channel_id=1, source_target_pairs={{16,0},{0,4},{24,8},{8,12},{20,16},{4,20},{28,24},{12,28},{17,1},{... | collective-permute-start | bytes 135176 | tf_op jit(solution)/shard_map/ppermute | solution.py:623
  197.7 7.7 %slice-start.1 = ((s8[5242880]{0:T(1024)(128)(4,1)}), s8[1048576]{0:T(1024)(128)(4,1)S(1)}, s32[]{:S(2)}) async-start(s8[5242880]{0:T(1024)(128)(4,1)} %bitcast.8), calls=%async_computation.1 | async-start | bytes 2097152
  197.7 3.5 %collective-permute-start.46 = (bf16[16,1408]{1,0:T(8,128)(2,1)S(1)}, bf16[16,1408]{1,0:T(8,128)(2,1)S(1)}, u32[]{:S(2)}, u32[]{:S(2)}) collective-permute-start(bf16[16,1408]{1,0:T(8,128)(2,1)S(1)} %get-tuple-element.134), channel_id=1, source_target_pairs={{24,0},{8,4},{16,8},{0,12},{28,16},{12,20},{20,24},{4,28},{25,1},{... | collective-permute-start | bytes 135176 | tf_op jit(solution)/shard_map/ppermute | solution.py:623
  202.4 1.4 collective-permute-start.47
  203.8 10.1 %collective-permute-start.48 = (bf16[32,1408]{1,0:T(8,128)(2,1)S(1)}, bf16[32,1408]{1,0:T(8,128)(2,1)S(1)}, u32[]{:S(2)}, u32[]{:S(2)}) collective-permute-start(bf16[32,1408]{1,0:T(8,128)(2,1)S(1)} %add_convert_fusion.mine_ref), channel_id=1, source_target_pairs={{0,16},{8,24},{16,0},{24,8},{1,17},{9,25},{17,1},{25,9},{2,18},{10... | collective-permute-start | bytes 270344 | tf_op jit(solution)/shard_map/ppermute | solution.py:631
  205.4 9.9 %copy-start.1 = (f32[1,2560]{1,0:T(1,128)S(1)}, f32[1,2560]{1,0:T(1,128)}, u32[]{:S(2)}) copy-start(f32[1,2560]{1,0:T(1,128)} %param.18) | copy-start | bytes 30724

commit v2 on v1

--- a/solution.py
+++ b/solution.py
@@ -329,16 +329,34 @@
     group = group or heads
 
     chunk = seq_dev // CHUNKS
+    several = heads // group
+    whole_tiles = group * head_size % LANES == 0
+    lane_groups = {k for k in range(several) if k % 5 in (1, 3)} if whole_tiles else set()
+
+    def lane_sums(values):
+        return jnp.sum(values.T, axis=0, keepdims=True)
 
     def work(c, at, carry):
         i = c * chunk + at
-        c_rows = jnp.broadcast_to(c_ref[pl.ds(i, 1), :], (SUBLANES, conv_c.shape[1]))
+        c_row = c_ref[pl.ds(i, 1), :]
+        c_rows = jnp.broadcast_to(c_row, (SUBLANES, conv_c.shape[1]))
         c_rows = c_rows.astype(jnp.bfloat16)
         found = []
         for first in range(0, heads, group):
             state = held_refs[c][at, first : first + group]
-            state = state.reshape(group * head_size, state.shape[2]).astype(jnp.bfloat16)
-            found.append(against(c_rows, state))
+            state = state.reshape(group * head_size, state.shape[2])
+            if first // group in lane_groups:
+                found.append(
+                    jnp.concatenate(
+                        [
+                            lane_sums(state[k : k + LANES] * c_row)
+                            for k in range(0, group * head_size, LANES)
+                        ],
+                        axis=1,
+                    )
+                )
+            else:
+                found.append(against(c_rows, state.astype(jnp.bfloat16)))
         tile = pl.ds(pl.multiple_of(i // SUBLANES * SUBLANES, SUBLANES), SUBLANES)
         width = group * head_size
         mine = lax.broadcasted_iota(jnp.int32, (SUBLANES, width), 0) == i % SUBLANES
@@ -638,10 +656,6 @@
     place = jnp.stack([target_index, mp_index, source_index, dp_index, section_index]).astype(jnp.int32)
 
     met = across(hidden_in, group)
-    first_half = dp_index < group
-    hidden = jnp.concatenate(
-        [jnp.where(first_half, hidden_in, met), jnp.where(first_half, met, hidden_in)], axis=0
-    )
     smalls = [w_bcdt[0]] + [across(w_bcdt[0], blocks * r) for r in range(1, dp_count // blocks)]
     gain_share = lax.dynamic_slice_in_dim(norm_gain, mp_index * model_share, model_share, 1)
     table = jnp.concatenate(
@@ -652,8 +666,12 @@
         ],
         axis=0,
     )
+    first_half = jnp.broadcast_to(dp_index < group, (seq_dev, model_share))
+    place, gain_share, first_half, local_slots = lax.optimization_barrier(
+        (place, gain_share, first_half, slots - dp_index * slots_dev)
+    )
     *held, w, past_x, past_bc, wide, head, now_bc, alive = load(
-        slots - dp_index * slots_dev,
+        local_slots,
         lengths,
         state_pool,
         w_zxo,
@@ -663,6 +681,10 @@
         jnp.concatenate([dt_bias, a_rate, skip_gain], axis=0),
     )
 
+    met, alive = lax.optimization_barrier((met, alive))
+    hidden = jnp.concatenate(
+        [jnp.where(first_half, hidden_in, met), jnp.where(first_half, met, hidden_in)], axis=0
+    )
     mine = []
     own = []
     for tick in range(section_count):

time: 216 us -> 207 us (0.958)
  Pallas kernels: 63.4 us -> 59.1 us
  waiting for transfers between devices: 71 us -> 67.5 us
    pallas_call x4, Pallas kernels: 25.6 us -> 21.3 us  [mix(): pl.pallas_call(functools.partial(mix_kernel, tick, rounds, parts, mp_coun...]
    ppermute x14, waiting for transfers between devices: 22.7 us -> 19.2 us  [across(): return lax.ppermute(array, 'dp', [(d, d ^ by) for d in range(dp_count)])]
    unnamed x20 -> x22, local copies, waits for them, and re-layouts: 6.23 us -> 6.23 us
  transfers between devices with their start and end apart: 49 -> 49, of which waited for: 29 -> 29; matrix products, arithmetic and copies ran while one was open for 1% -> 1% of each run, Pallas kernels for 8% -> 9%
where the time goes in v2:
time: 207 us; the launch traced here: 206 us
  starting transfers between devices  70.2 us (34%)
  waiting for transfers between devices  67.5 us (33%)
  Pallas kernels  59.1 us (29%)
  local copies, waits for them, and re-layouts  6.33 us (3%)
  other arithmetic  2.31 us (1%)
    ppermute x16, waiting for transfers between devices, to_heads(): lax.ppermute(piece, ('dp', 'mp'), forward_pairs(r))  30.2 us
    ppermute x16, starting transfers between devices, to_blocks(): lax.ppermute(piece, ('dp', 'mp'), [(b, a) for a, b in forward_pairs(r)])  25.6 us
    ppermute x16, starting transfers between devices, to_heads(): lax.ppermute(piece, ('dp', 'mp'), forward_pairs(r))  24.1 us
    pallas_call x4, Pallas kernels, mix(): pl.pallas_call(functools.partial(mix_kernel, tick, rounds, parts, mp_coun...  21.3 us
    ppermute x14, waiting for transfers between devices, across(): return lax.ppermute(array, 'dp', [(d, d ^ by) for d in range(dp_count)])  19.2 us
    ppermute x16, waiting for transfers between devices, to_blocks(): lax.ppermute(piece, ('dp', 'mp'), [(b, a) for a, b in forward_pairs(r)])  12.7 us
    pallas_call x4, Pallas kernels, project(): pl.pallas_call(functools.partial(project_kernel, parts, seq_dev, len(smal...  11.8 us
    ppermute x14, starting transfers between devices, across(): return lax.ppermute(array, 'dp', [(d, d ^ by) for d in range(dp_count)])  11 us
  transfers between devices with their start and end apart: 49, of which 29 were waited for; matrix products, arithmetic and copies ran while one was open for 1% of the time, Pallas kernels for 9%

profile of v2, /device:TPU:0, one launch (start us, length us, event | category | flops | bytes accessed | tf_op | source)
XLA Modules:
  0.0 206.4 jit_solution(8121912447329023826)
XLA Ops:
  0.6 3.1 %collective-permute-start = (bf16[16,1280]{1,0:T(8,128)(2,1)}, bf16[16,1280]{1,0:T(8,128)(2,1)S(1)}, u32[]{:S(2)}, u32[]{:S(2)}) collective-permute-start(bf16[16,1280]{1,0:T(8,128)(2,1)} %param.15), channel_id=1, source_target_pairs={{0,16},{8,24},{16,0},{24,8},{1,17},{9,25},{17,1},{25,9},{2,18},{10... | collective-permute-start | bytes 122888 | tf_op jit(solution)/shard_map/ppermute | solution.py:649
  4.5 0.8 fusion.table_ref
  6.1 3.8 %copy-done.3 = bf16[1,3,1280,1280]{3,2,1,0:T(8,128)(2,1)S(1)} copy-done((bf16[1,3,1280,1280]{3,2,1,0:T(8,128)(2,1)S(1)}, bf16[1,3,1280,1280]{3,2,1,0:T(8,128)(2,1)}, u32[]{:S(2)}) %copy-start.3) | copy-done | bytes 9830424
  9.9 1.0 copy-done.5
  12.3 9.2 %load.1 = (f32[4,40,64,128]{3,2,1,0:T(8,128)S(1)}, f32[4,40,64,128]{3,2,1,0:T(8,128)S(1)}, f32[4,40,64,128]{3,2,1,0:T(8,128)S(1)}, f32[4,40,64,128]{3,2,1,0:T(8,...) custom-call(s32[16]{0:T(128)S(1)} %broadcast_subtract_fusion.slots_r, ...), custom_call_target="tpu_custom_call" | custom-call | flops 83886080 | bytes 30801920 | tf_op jit(solution)/shard_map/load/pallas_call | solution.py:163
  21.7 1.3 collective-permute-done.2.refs_3_
  22.9 3.0 %project.4 = (bf16[16,3072]{1,0:T(8,128)(2,1)S(1)}, bf16[16,3072]{1,0:T(8,128)(2,1)S(1)}, bf16[16,3072]{1,0:T(8,128)(2,1)S(1)}, bf16[16,3072]{1,0:T(8,128)(2,1)S(1)}) custom-call(s32[5]{0:T(128)S(1)} %stack.20.place_ref, f32[1,1280]{1,0:T(1,128)S(1)} %constant_dynamic-slice_fusion.gain_ref, bf16[3,1280,1280]{2,1,0:T(8,128)(2,1)S(1)} %get-tuple-element.80.w_ref, ...), custom_call_target="tpu_custom_call" | custom-call | flops 482344960 | bytes 7536640 | tf_op jit(solution)/shard_map/project/pallas_call | solution.py:251
  26.8 5.4 %collective-permute-start.5 = (bf16[16,3072]{1,0:T(8,128)(2,1)S(1)}, bf16[16,3072]{1,0:T(8,128)(2,1)S(1)}, u32[]{:S(2)}, u32[]{:S(2)}) collective-permute-start(bf16[16,3072]{1,0:T(8,128)(2,1)S(1)} %get-tuple-element.97), channel_id=1, source_target_pairs={{0,16},{4,0},{8,24},{12,8},{16,20},{20,4},{24,28},{28,12},{1,17},{... | collective-permute-start | bytes 294920 | tf_op jit(solution)/shard_map/ppermute | solution.py:636
  32.5 6.1 %collective-permute-done.5.refs_6_ = bf16[16,3072]{1,0:T(8,128)(2,1)S(1)} collective-permute-done((bf16[16,3072]{1,0:T(8,128)(2,1)S(1)}, bf16[16,3072]{1,0:T(8,128)(2,1)S(1)}, u32[]{:S(2)}, u32[]{:S(2)}) %collective-permute-start.5) | collective-permute-done | bytes 98336 | tf_op jit(solution)/shard_map/ppermute | solution.py:636
  38.6 1.4 collective-permute-done.6.refs_7_
  40.0 5.3 %mix.4 = (bf16[16,1408]{1,0:T(8,128)(2,1)S(1)}, bf16[16,1408]{1,0:T(8,128)(2,1)S(1)}, bf16[16,1408]{1,0:T(8,128)(2,1)S(1)}, bf16[16,1408]{1,0:T(8,128)(2,1)S(1)}...) custom-call(s32[5]{0:T(128)S(1)} %stack.20.place_ref, ...), custom_call_target="tpu_custom_call" | custom-call | flops 83886080 | bytes 20971520 | tf_op jit(solution)/shard_map/mix/pallas_call | solution.py:412
  46.2 5.2 %collective-permute-start.9 = (bf16[16,1408]{1,0:T(8,128)(2,1)S(1)}, bf16[16,1408]{1,0:T(8,128)(2,1)S(1)}, u32[]{:S(2)}, u32[]{:S(2)}) collective-permute-start(bf16[16,1408]{1,0:T(8,128)(2,1)S(1)} %get-tuple-element.101), channel_id=1, source_target_pairs={{16,0},{0,4},{24,8},{8,12},{20,16},{4,20},{28,24},{12,28},{17,1},{... | collective-permute-start | bytes 135176 | tf_op jit(solution)/shard_map/ppermute | solution.py:641
  51.7 2.2 %collective-permute-done.9.refs_2_ = bf16[16,1408]{1,0:T(8,128)(2,1)S(1)} collective-permute-done((bf16[16,1408]{1,0:T(8,128)(2,1)S(1)}, bf16[16,1408]{1,0:T(8,128)(2,1)S(1)}, u32[]{:S(2)}, u32[]{:S(2)}) %collective-permute-start.9) | collective-permute-done | bytes 45088 | tf_op jit(solution)/shard_map/ppermute | solution.py:641
  53.9 1.0 collective-permute-done.10.refs_3_
  54.9 1.2 finish.4
  56.6 0.9 collective-permute-done.11
  57.5 1.5 collective-permute-start.12
  59.0 3.5 %collective-permute-done.12.met_ref = bf16[32,1408]{1,0:T(8,128)(2,1)S(1)} collective-permute-done((bf16[32,1408]{1,0:T(8,128)(2,1)S(1)}, bf16[32,1408]{1,0:T(8,128)(2,1)S(1)}, u32[]{:S(2)}, u32[]{:S(2)}) %collective-permute-start.12) | collective-permute-done | bytes 90144 | tf_op jit(solution)/shard_map/ppermute | solution.py:649
  63.1 1.6 collective-permute-start.13
  64.8 2.9 %collective-permute-done.13.refs_2_.old_ref = bf16[32,1280]{1,0:T(8,128)(2,1)S(1)} collective-permute-done((bf16[32,1280]{1,0:T(8,128)(2,1)S(1)}, bf16[32,1280]{1,0:T(8,128)(2,1)S(1)}, u32[]{:S(2)}, u32[]{:S(2)}) %collective-permute-start.13) | collective-permute-done | bytes 81952 | tf_op jit(solution)/shard_map/ppermute | solution.py:734
  67.6 1.3 collective-permute-done.14.refs_3_
  68.9 2.9 %project.5 = (bf16[16,3072]{1,0:T(8,128)(2,1)S(1)}, bf16[16,3072]{1,0:T(8,128)(2,1)S(1)}, bf16[16,3072]{1,0:T(8,128)(2,1)S(1)}, bf16[16,3072]{1,0:T(8,128)(2,1)S(1)}) custom-call(s32[5]{0:T(128)S(1)} %stack.20.place_ref, f32[1,1280]{1,0:T(1,128)S(1)} %constant_dynamic-slice_fusion.gain_ref, bf16[3,1280,1280]{2,1,0:T(8,128)(2,1)S(1)} %get-tuple-element.80.w_ref, ...), custom_call_target="tpu_custom_call" | custom-call | flops 482344960 | bytes 7536640 | tf_op jit(solution)/shard_map/project/pallas_call | solution.py:251
  72.8 4.7 %collective-permute-start.17 = (bf16[16,3072]{1,0:T(8,128)(2,1)S(1)}, bf16[16,3072]{1,0:T(8,128)(2,1)S(1)}, u32[]{:S(2)}, u32[]{:S(2)}) collective-permute-start(bf16[16,3072]{1,0:T(8,128)(2,1)S(1)} %get-tuple-element.108), channel_id=1, source_target_pairs={{0,16},{4,0},{8,24},{12,8},{16,20},{20,4},{24,28},{28,12},{1,17},{... | collective-permute-start | bytes 294920 | tf_op jit(solution)/shard_map/ppermute | solution.py:636
  77.7 6.1 %collective-permute-done.17.refs_6_ = bf16[16,3072]{1,0:T(8,128)(2,1)S(1)} collective-permute-done((bf16[16,3072]{1,0:T(8,128)(2,1)S(1)}, bf16[16,3072]{1,0:T(8,128)(2,1)S(1)}, u32[]{:S(2)}, u32[]{:S(2)}) %collective-permute-start.17) | collective-permute-done | bytes 98336 | tf_op jit(solution)/shard_map/ppermute | solution.py:636
  83.9 1.4 collective-permute-done.18.refs_7_
  85.3 5.3 %mix.5 = (bf16[16,1408]{1,0:T(8,128)(2,1)S(1)}, bf16[16,1408]{1,0:T(8,128)(2,1)S(1)}, bf16[16,1408]{1,0:T(8,128)(2,1)S(1)}, bf16[16,1408]{1,0:T(8,128)(2,1)S(1)}...) custom-call(s32[5]{0:T(128)S(1)} %stack.20.place_ref, ...), custom_call_target="tpu_custom_call" | custom-call | flops 83886080 | bytes 20971520 | tf_op jit(solution)/shard_map/mix/pallas_call | solution.py:412
  91.5 5.2 %collective-permute-start.21 = (bf16[16,1408]{1,0:T(8,128)(2,1)S(1)}, bf16[16,1408]{1,0:T(8,128)(2,1)S(1)}, u32[]{:S(2)}, u32[]{:S(2)}) collective-permute-start(bf16[16,1408]{1,0:T(8,128)(2,1)S(1)} %get-tuple-element.115), channel_id=1, source_target_pairs={{16,0},{0,4},{24,8},{8,12},{20,16},{4,20},{28,24},{12,28},{17,1},{... | collective-permute-start | bytes 135176 | tf_op jit(solution)/shard_map/ppermute | solution.py:641
  97.0 2.2 %collective-permute-done.21.refs_2_ = bf16[16,1408]{1,0:T(8,128)(2,1)S(1)} collective-permute-done((bf16[16,1408]{1,0:T(8,128)(2,1)S(1)}, bf16[16,1408]{1,0:T(8,128)(2,1)S(1)}, u32[]{:S(2)}, u32[]{:S(2)}) %collective-permute-start.21) | collective-permute-done | bytes 45088 | tf_op jit(solution)/shard_map/ppermute | solution.py:641
  99.2 1.0 collective-permute-done.22.refs_3_
  100.1 1.2 finish.5
  101.8 0.9 collective-permute-done.23
  102.8 1.5 collective-permute-start.24
  104.3 3.5 %collective-permute-done.24.met_ref = bf16[32,1408]{1,0:T(8,128)(2,1)S(1)} collective-permute-done((bf16[32,1408]{1,0:T(8,128)(2,1)S(1)}, bf16[32,1408]{1,0:T(8,128)(2,1)S(1)}, u32[]{:S(2)}, u32[]{:S(2)}) %collective-permute-start.24) | collective-permute-done | bytes 90144 | tf_op jit(solution)/shard_map/ppermute | solution.py:649
  108.4 0.8 collective-permute-start.25
  109.3 1.3 collective-permute-done.26.refs_3_
  110.6 2.9 %project.6 = (bf16[16,3072]{1,0:T(8,128)(2,1)S(1)}, bf16[16,3072]{1,0:T(8,128)(2,1)S(1)}, bf16[16,3072]{1,0:T(8,128)(2,1)S(1)}, bf16[16,3072]{1,0:T(8,128)(2,1)S(1)}) custom-call(s32[5]{0:T(128)S(1)} %stack.20.place_ref, f32[1,1280]{1,0:T(1,128)S(1)} %constant_dynamic-slice_fusion.gain_ref, bf16[3,1280,1280]{2,1,0:T(8,128)(2,1)S(1)} %get-tuple-element.80.w_ref, ...), custom_call_target="tpu_custom_call" | custom-call | flops 482344960 | bytes 7536640 | tf_op jit(solution)/shard_map/project/pallas_call | solution.py:251
  114.5 4.7 %collective-permute-start.29 = (bf16[16,3072]{1,0:T(8,128)(2,1)S(1)}, bf16[16,3072]{1,0:T(8,128)(2,1)S(1)}, u32[]{:S(2)}, u32[]{:S(2)}) collective-permute-start(bf16[16,3072]{1,0:T(8,128)(2,1)S(1)} %get-tuple-element.123), channel_id=1, source_target_pairs={{0,16},{4,0},{8,24},{12,8},{16,20},{20,4},{24,28},{28,12},{1,17},{... | collective-permute-start | bytes 294920 | tf_op jit(solution)/shard_map/ppermute | solution.py:636
  119.4 6.1 %collective-permute-done.29.refs_6_ = bf16[16,3072]{1,0:T(8,128)(2,1)S(1)} collective-permute-done((bf16[16,3072]{1,0:T(8,128)(2,1)S(1)}, bf16[16,3072]{1,0:T(8,128)(2,1)S(1)}, u32[]{:S(2)}, u32[]{:S(2)}) %collective-permute-start.29) | collective-permute-done | bytes 98336 | tf_op jit(solution)/shard_map/ppermute | solution.py:636
  125.5 1.4 collective-permute-done.30.refs_7_
  127.0 5.3 %mix.6 = (bf16[16,1408]{1,0:T(8,128)(2,1)S(1)}, bf16[16,1408]{1,0:T(8,128)(2,1)S(1)}, bf16[16,1408]{1,0:T(8,128)(2,1)S(1)}, bf16[16,1408]{1,0:T(8,128)(2,1)S(1)}...) custom-call(s32[5]{0:T(128)S(1)} %stack.20.place_ref, ...), custom_call_target="tpu_custom_call" | custom-call | flops 83886080 | bytes 20971520 | tf_op jit(solution)/shard_map/mix/pallas_call | solution.py:412
  133.2 5.2 %collective-permute-start.33 = (bf16[16,1408]{1,0:T(8,128)(2,1)S(1)}, bf16[16,1408]{1,0:T(8,128)(2,1)S(1)}, u32[]{:S(2)}, u32[]{:S(2)}) collective-permute-start(bf16[16,1408]{1,0:T(8,128)(2,1)S(1)} %get-tuple-element.130), channel_id=1, source_target_pairs={{16,0},{0,4},{24,8},{8,12},{20,16},{4,20},{28,24},{12,28},{17,1},{... | collective-permute-start | bytes 135176 | tf_op jit(solution)/shard_map/ppermute | solution.py:641
  138.7 2.2 %collective-permute-done.33.refs_2_ = bf16[16,1408]{1,0:T(8,128)(2,1)S(1)} collective-permute-done((bf16[16,1408]{1,0:T(8,128)(2,1)S(1)}, bf16[16,1408]{1,0:T(8,128)(2,1)S(1)}, u32[]{:S(2)}, u32[]{:S(2)}) %collective-permute-start.33) | collective-permute-done | bytes 45088 | tf_op jit(solution)/shard_map/ppermute | solution.py:641
  140.9 1.0 collective-permute-done.34.refs_3_
  141.8 1.2 finish.6
  143.5 0.9 collective-permute-done.35
  144.5 1.5 collective-permute-start.36
  146.0 3.5 %collective-permute-done.36.met_ref = bf16[32,1408]{1,0:T(8,128)(2,1)S(1)} collective-permute-done((bf16[32,1408]{1,0:T(8,128)(2,1)S(1)}, bf16[32,1408]{1,0:T(8,128)(2,1)S(1)}, u32[]{:S(2)}, u32[]{:S(2)}) %collective-permute-start.36) | collective-permute-done | bytes 90144 | tf_op jit(solution)/shard_map/ppermute | solution.py:649
  150.1 7.1 %collective-permute-start.37 = (bf16[32,1280]{1,0:T(8,128)(2,1)S(1)}, bf16[32,1280]{1,0:T(8,128)(2,1)S(1)}, u32[]{:S(2)}, u32[]{:S(2)}) collective-permute-start(bf16[32,1280]{1,0:T(8,128)(2,1)S(1)} %get-tuple-element.135), channel_id=1, source_target_pairs={{0,1},{1,0},{2,3},{3,2},{4,5},{5,4},{6,7},{7,6},{8,9},{9,8},{10,11... | collective-permute-start | bytes 245768 | tf_op jit(solution)/shard_map/ppermute | solution.py:734
  157.1 2.4 %collective-permute-done.37.refs_2_.old_ref = bf16[32,1280]{1,0:T(8,128)(2,1)S(1)} collective-permute-done((bf16[32,1280]{1,0:T(8,128)(2,1)S(1)}, bf16[32,1280]{1,0:T(8,128)(2,1)S(1)}, u32[]{:S(2)}, u32[]{:S(2)}) %collective-permute-start.37) | collective-permute-done | bytes 81952 | tf_op jit(solution)/shard_map/ppermute | solution.py:734
  159.6 1.3 collective-permute-done.38.refs_3_
  160.8 2.9 %project.7 = (bf16[16,3072]{1,0:T(8,128)(2,1)S(1)}, bf16[16,3072]{1,0:T(8,128)(2,1)S(1)}, bf16[16,3072]{1,0:T(8,128)(2,1)S(1)}, bf16[16,3072]{1,0:T(8,128)(2,1)S(1)}) custom-call(s32[5]{0:T(128)S(1)} %stack.20.place_ref, f32[1,1280]{1,0:T(1,128)S(1)} %constant_dynamic-slice_fusion.gain_ref, bf16[3,1280,1280]{2,1,0:T(8,128)(2,1)S(1)} %get-tuple-element.80.w_ref, ...), custom_call_target="tpu_custom_call" | custom-call | flops 482344960 | bytes 7536640 | tf_op jit(solution)/shard_map/project/pallas_call | solution.py:251
  164.7 4.7 %collective-permute-start.41 = (bf16[16,3072]{1,0:T(8,128)(2,1)S(1)}, bf16[16,3072]{1,0:T(8,128)(2,1)S(1)}, u32[]{:S(2)}, u32[]{:S(2)}) collective-permute-start(bf16[16,3072]{1,0:T(8,128)(2,1)S(1)} %get-tuple-element.138), channel_id=1, source_target_pairs={{0,16},{4,0},{8,24},{12,8},{16,20},{20,4},{24,28},{28,12},{1,17},{... | collective-permute-start | bytes 294920 | tf_op jit(solution)/shard_map/ppermute | solution.py:636
  169.6 6.1 %collective-permute-done.41.refs_6_ = bf16[16,3072]{1,0:T(8,128)(2,1)S(1)} collective-permute-done((bf16[16,3072]{1,0:T(8,128)(2,1)S(1)}, bf16[16,3072]{1,0:T(8,128)(2,1)S(1)}, u32[]{:S(2)}, u32[]{:S(2)}) %collective-permute-start.41) | collective-permute-done | bytes 98336 | tf_op jit(solution)/shard_map/ppermute | solution.py:636
  175.8 1.4 collective-permute-done.42.refs_7_
  177.2 5.3 %mix.7 = (bf16[16,1408]{1,0:T(8,128)(2,1)S(1)}, bf16[16,1408]{1,0:T(8,128)(2,1)S(1)}, bf16[16,1408]{1,0:T(8,128)(2,1)S(1)}, bf16[16,1408]{1,0:T(8,128)(2,1)S(1)}...) custom-call(s32[5]{0:T(128)S(1)} %stack.20.place_ref, ...), custom_call_target="tpu_custom_call" | custom-call | flops 83886080 | bytes 20971520 | tf_op jit(solution)/shard_map/mix/pallas_call | solution.py:412
  182.5 0.8 collective-permute-start.43
  183.6 5.3 %collective-permute-start.45 = (bf16[16,1408]{1,0:T(8,128)(2,1)S(1)}, bf16[16,1408]{1,0:T(8,128)(2,1)S(1)}, u32[]{:S(2)}, u32[]{:S(2)}) collective-permute-start(bf16[16,1408]{1,0:T(8,128)(2,1)S(1)} %get-tuple-element.145), channel_id=1, source_target_pairs={{16,0},{0,4},{24,8},{8,12},{20,16},{4,20},{28,24},{12,28},{17,1},{... | collective-permute-start | bytes 135176 | tf_op jit(solution)/shard_map/ppermute | solution.py:641
  189.2 2.2 %collective-permute-done.45.refs_2_ = bf16[16,1408]{1,0:T(8,128)(2,1)S(1)} collective-permute-done((bf16[16,1408]{1,0:T(8,128)(2,1)S(1)}, bf16[16,1408]{1,0:T(8,128)(2,1)S(1)}, u32[]{:S(2)}, u32[]{:S(2)}) %collective-permute-start.45) | collective-permute-done | bytes 45088 | tf_op jit(solution)/shard_map/ppermute | solution.py:641
  191.4 1.0 collective-permute-done.46.refs_3_
  192.3 1.2 finish.7
  194.0 0.9 collective-permute-done.47
  195.0 1.5 collective-permute-start.48
  196.5 8.6 %write_states.1 = f32[1,16,40,64,128]{4,3,2,1,0:T(8,128)} custom-call(f32[16,40]{1,0:T(8,128)S(1)} %get-tuple-element.151.decay_ref, f32[16,2560]{1,0:T(8,128)S(1)} %get-tuple-element.152.x_ref, f32[16,128]{1,0:T(8,128)S(1)} %get-tuple-element.153.b_ref, f32[4,40,64,128]{3,2,1,0:T(8,128)S(1)} %get-tuple-element.88.refs_0_, ...), custom_call_target="tpu_custom_call" | custom-call | flops 83886080 | bytes 41943040 | tf_op jit(solution)/shard_map/write_states/pallas_call | solution.py:558
  205.1 1.3 settle.7
  (87 shorter events, 15.6 us)
Async XLA Ops:
  0.6 3.2 %copy-start = (f32[1,2560]{1,0:T(1,128)S(1)}, f32[1,2560]{1,0:T(1,128)}, u32[]{:S(2)}) copy-start(f32[1,2560]{1,0:T(1,128)} %param.18) | copy-start | bytes 30724
  0.6 20.9 %collective-permute-start = (bf16[16,1280]{1,0:T(8,128)(2,1)}, bf16[16,1280]{1,0:T(8,128)(2,1)S(1)}, u32[]{:S(2)}, u32[]{:S(2)}) collective-permute-start(bf16[16,1280]{1,0:T(8,128)(2,1)} %param.15), channel_id=1, source_target_pairs={{0,16},{8,24},{16,0},{24,8},{1,17},{9,25},{17,1},{25,9},{2,18},{10... | collective-permute-start | bytes 122888 | tf_op jit(solution)/shard_map/ppermute | solution.py:649
  3.7 19.2 %collective-permute-start.1 = (bf16[84,1280]{1,0:T(8,128)(2,1)}, bf16[84,1280]{1,0:T(8,128)(2,1)S(1)}, u32[]{:S(2)}, u32[]{:S(2)}) collective-permute-start(bf16[84,1280]{1,0:T(8,128)(2,1)} %bitcast.10), channel_id=1, source_target_pairs={{0,16},{8,24},{16,0},{24,8},{1,17},{9,25},{17,1},{25,9},{2,18},{10... | collective-permute-start | bytes 645128 | tf_op jit(solution)/shard_map/ppermute | solution.py:649
  6.1 3.8 %copy-start.3 = (bf16[1,3,1280,1280]{3,2,1,0:T(8,128)(2,1)S(1)}, bf16[1,3,1280,1280]{3,2,1,0:T(8,128)(2,1)}, u32[]{:S(2)}) copy-start(bf16[1,3,1280,1280]{3,2,1,0:T(8,128)(2,1)} %w_ref.1) | copy-start | bytes 29491204
  9.9 1.0 copy-start.5
  10.9 0.8 copy-start.6
  11.6 0.7 copy-start.7
  12.3 9.3 %copy-start.8 = (bf16[16,1280]{1,0:T(8,128)(2,1)S(1)}, bf16[16,1280]{1,0:T(8,128)(2,1)}, u32[]{:S(2)}) copy-start(bf16[16,1280]{1,0:T(8,128)(2,1)} %param.15) | copy-start | bytes 122884
  12.3 10.6 %copy-start.4 = (bf16[1,84,1280]{2,1,0:T(8,128)(2,1)S(1)}, bf16[1,84,1280]{2,1,0:T(8,128)(2,1)}, u32[]{:S(2)}) copy-start(bf16[1,84,1280]{2,1,0:T(8,128)(2,1)} %param.20) | copy-start | bytes 645124
  21.5 155.7 %copy-start.2 = (f32[4,40,64,128]{3,2,1,0:T(8,128)}, f32[4,40,64,128]{3,2,1,0:T(8,128)S(1)}, u32[]{:S(2)}) copy-start(f32[4,40,64,128]{3,2,1,0:T(8,128)S(1)} %get-tuple-element.91.refs_3_) | copy-start | bytes 15728644
  21.6 1.3 collective-permute-start.2
  25.9 6.6 %collective-permute-start.3 = (bf16[16,3072]{1,0:T(8,128)(2,1)S(1)}, bf16[16,3072]{1,0:T(8,128)(2,1)S(1)}, u32[]{:S(2)}, u32[]{:S(2)}) collective-permute-start(bf16[16,3072]{1,0:T(8,128)(2,1)S(1)} %get-tuple-element.95), channel_id=1, source_target_pairs={{0,0},{4,16},{8,8},{12,24},{16,4},{20,20},{24,12},{28,28},{1,1},{5... | collective-permute-start | bytes 294920 | tf_op jit(solution)/shard_map/ppermute | solution.py:636
  26.6 5.9 %collective-permute-start.4 = (bf16[16,3072]{1,0:T(8,128)(2,1)S(1)}, bf16[16,3072]{1,0:T(8,128)(2,1)S(1)}, u32[]{:S(2)}, u32[]{:S(2)}) collective-permute-start(bf16[16,3072]{1,0:T(8,128)(2,1)S(1)} %get-tuple-element.96), channel_id=1, source_target_pairs={{0,8},{4,24},{8,0},{12,16},{16,12},{20,28},{24,4},{28,20},{1,9},{5... | collective-permute-start | bytes 294920 | tf_op jit(solution)/shard_map/ppermute | solution.py:636
  26.8 11.8 %collective-permute-start.5 = (bf16[16,3072]{1,0:T(8,128)(2,1)S(1)}, bf16[16,3072]{1,0:T(8,128)(2,1)S(1)}, u32[]{:S(2)}, u32[]{:S(2)}) collective-permute-start(bf16[16,3072]{1,0:T(8,128)(2,1)S(1)} %get-tuple-element.97), channel_id=1, source_target_pairs={{0,16},{4,0},{8,24},{12,8},{16,20},{20,4},{24,28},{28,12},{1,17},{... | collective-permute-start | bytes 294920 | tf_op jit(solution)/shard_map/ppermute | solution.py:636
  32.2 7.8 %collective-permute-start.6 = (bf16[16,3072]{1,0:T(8,128)(2,1)S(1)}, bf16[16,3072]{1,0:T(8,128)(2,1)S(1)}, u32[]{:S(2)}, u32[]{:S(2)}) collective-permute-start(bf16[16,3072]{1,0:T(8,128)(2,1)S(1)} %get-tuple-element.98), channel_id=1, source_target_pairs={{0,24},{4,8},{8,16},{12,0},{16,28},{20,12},{24,20},{28,4},{1,25},{... | collective-permute-start | bytes 294920 | tf_op jit(solution)/shard_map/ppermute | solution.py:636
  45.3 6.4 %collective-permute-start.7 = (bf16[16,1408]{1,0:T(8,128)(2,1)S(1)}, bf16[16,1408]{1,0:T(8,128)(2,1)S(1)}, u32[]{:S(2)}, u32[]{:S(2)}) collective-permute-start(bf16[16,1408]{1,0:T(8,128)(2,1)S(1)} %get-tuple-element.99), channel_id=1, source_target_pairs={{0,0},{16,4},{8,8},{24,12},{4,16},{20,20},{12,24},{28,28},{1,1},{1... | collective-permute-start | bytes 135176 | tf_op jit(solution)/shard_map/ppermute | solution.py:641
  46.0 5.7 %collective-permute-start.8 = (bf16[16,1408]{1,0:T(8,128)(2,1)S(1)}, bf16[16,1408]{1,0:T(8,128)(2,1)S(1)}, u32[]{:S(2)}, u32[]{:S(2)}) collective-permute-start(bf16[16,1408]{1,0:T(8,128)(2,1)S(1)} %get-tuple-element.100), channel_id=1, source_target_pairs={{8,0},{24,4},{0,8},{16,12},{12,16},{28,20},{4,24},{20,28},{9,1},{2... | collective-permute-start | bytes 135176 | tf_op jit(solution)/shard_map/ppermute | solution.py:641
  46.2 7.7 %collective-permute-start.9 = (bf16[16,1408]{1,0:T(8,128)(2,1)S(1)}, bf16[16,1408]{1,0:T(8,128)(2,1)S(1)}, u32[]{:S(2)}, u32[]{:S(2)}) collective-permute-start(bf16[16,1408]{1,0:T(8,128)(2,1)S(1)} %get-tuple-element.101), channel_id=1, source_target_pairs={{16,0},{0,4},{24,8},{8,12},{20,16},{4,20},{28,24},{12,28},{17,1},{... | collective-permute-start | bytes 135176 | tf_op jit(solution)/shard_map/ppermute | solution.py:641
  51.4 3.5 %collective-permute-start.10 = (bf16[16,1408]{1,0:T(8,128)(2,1)S(1)}, bf16[16,1408]{1,0:T(8,128)(2,1)S(1)}, u32[]{:S(2)}, u32[]{:S(2)}) collective-permute-start(bf16[16,1408]{1,0:T(8,128)(2,1)S(1)} %get-tuple-element.102), channel_id=1, source_target_pairs={{24,0},{8,4},{16,8},{0,12},{28,16},{12,20},{20,24},{4,28},{25,1},{... | collective-permute-start | bytes 135176 | tf_op jit(solution)/shard_map/ppermute | solution.py:641
  56.1 1.4 collective-permute-start.11
  57.5 4.9 %collective-permute-start.12 = (bf16[32,1408]{1,0:T(8,128)(2,1)S(1)}, bf16[32,1408]{1,0:T(8,128)(2,1)S(1)}, u32[]{:S(2)}, u32[]{:S(2)}) collective-permute-start(bf16[32,1408]{1,0:T(8,128)(2,1)S(1)} %add_convert_fusion.3.mine_ref), channel_id=1, source_target_pairs={{0,16},{8,24},{16,0},{24,8},{1,17},{9,25},{17,1},{25,9},{2,18},{10... | collective-permute-start | bytes 270344 | tf_op jit(solution)/shard_map/ppermute | solution.py:649
  63.1 4.5 %collective-permute-start.13 = (bf16[32,1280]{1,0:T(8,128)(2,1)S(1)}, bf16[32,1280]{1,0:T(8,128)(2,1)S(1)}, u32[]{:S(2)}, u32[]{:S(2)}) collective-permute-start(bf16[32,1280]{1,0:T(8,128)(2,1)S(1)} %get-tuple-element.105), channel_id=1, source_target_pairs={{0,1},{1,0},{2,3},{3,2},{4,5},{5,4},{6,7},{7,6},{8,9},{9,8},{10,11... | collective-permute-start | bytes 245768 | tf_op jit(solution)/shard_map/ppermute | solution.py:734
  67.6 1.3 collective-permute-start.14
  71.9 5.9 %collective-permute-start.15 = (bf16[16,3072]{1,0:T(8,128)(2,1)S(1)}, bf16[16,3072]{1,0:T(8,128)(2,1)S(1)}, u32[]{:S(2)}, u32[]{:S(2)}) collective-permute-start(bf16[16,3072]{1,0:T(8,128)(2,1)S(1)} %get-tuple-element.106), channel_id=1, source_target_pairs={{0,0},{4,16},{8,8},{12,24},{16,4},{20,20},{24,12},{28,28},{1,1},{5... | collective-permute-start | bytes 294920 | tf_op jit(solution)/shard_map/ppermute | solution.py:636
  72.5 5.2 %collective-permute-start.16 = (bf16[16,3072]{1,0:T(8,128)(2,1)S(1)}, bf16[16,3072]{1,0:T(8,128)(2,1)S(1)}, u32[]{:S(2)}, u32[]{:S(2)}) collective-permute-start(bf16[16,3072]{1,0:T(8,128)(2,1)S(1)} %get-tuple-element.107), channel_id=1, source_target_pairs={{0,8},{4,24},{8,0},{12,16},{16,12},{20,28},{24,4},{28,20},{1,9},{5... | collective-permute-start | bytes 294920 | tf_op jit(solution)/shard_map/ppermute | solution.py:636
  72.8 11.1 %collective-permute-start.17 = (bf16[16,3072]{1,0:T(8,128)(2,1)S(1)}, bf16[16,3072]{1,0:T(8,128)(2,1)S(1)}, u32[]{:S(2)}, u32[]{:S(2)}) collective-permute-start(bf16[16,3072]{1,0:T(8,128)(2,1)S(1)} %get-tuple-element.108), channel_id=1, source_target_pairs={{0,16},{4,0},{8,24},{12,8},{16,20},{20,4},{24,28},{28,12},{1,17},{... | collective-permute-start | bytes 294920 | tf_op jit(solution)/shard_map/ppermute | solution.py:636
  77.5 7.8 %collective-permute-start.18 = (bf16[16,3072]{1,0:T(8,128)(2,1)S(1)}, bf16[16,3072]{1,0:T(8,128)(2,1)S(1)}, u32[]{:S(2)}, u32[]{:S(2)}) collective-permute-start(bf16[16,3072]{1,0:T(8,128)(2,1)S(1)} %get-tuple-element.109), channel_id=1, source_target_pairs={{0,24},{4,8},{8,16},{12,0},{16,28},{20,12},{24,20},{28,4},{1,25},{... | collective-permute-start | bytes 294920 | tf_op jit(solution)/shard_map/ppermute | solution.py:636
  90.6 6.4 %collective-permute-start.19 = (bf16[16,1408]{1,0:T(8,128)(2,1)S(1)}, bf16[16,1408]{1,0:T(8,128)(2,1)S(1)}, u32[]{:S(2)}, u32[]{:S(2)}) collective-permute-start(bf16[16,1408]{1,0:T(8,128)(2,1)S(1)} %get-tuple-element.113), channel_id=1, source_target_pairs={{0,0},{16,4},{8,8},{24,12},{4,16},{20,20},{12,24},{28,28},{1,1},{1... | collective-permute-start | bytes 135176 | tf_op jit(solution)/shard_map/ppermute | solution.py:641
  91.3 5.7 %collective-permute-start.20 = (bf16[16,1408]{1,0:T(8,128)(2,1)S(1)}, bf16[16,1408]{1,0:T(8,128)(2,1)S(1)}, u32[]{:S(2)}, u32[]{:S(2)}) collective-permute-start(bf16[16,1408]{1,0:T(8,128)(2,1)S(1)} %get-tuple-element.114), channel_id=1, source_target_pairs={{8,0},{24,4},{0,8},{16,12},{12,16},{28,20},{4,24},{20,28},{9,1},{2... | collective-permute-start | bytes 135176 | tf_op jit(solution)/shard_map/ppermute | solution.py:641
  91.5 7.7 %collective-permute-start.21 = (bf16[16,1408]{1,0:T(8,128)(2,1)S(1)}, bf16[16,1408]{1,0:T(8,128)(2,1)S(1)}, u32[]{:S(2)}, u32[]{:S(2)}) collective-permute-start(bf16[16,1408]{1,0:T(8,128)(2,1)S(1)} %get-tuple-element.115), channel_id=1, source_target_pairs={{16,0},{0,4},{24,8},{8,12},{20,16},{4,20},{28,24},{12,28},{17,1},{... | collective-permute-start | bytes 135176 | tf_op jit(solution)/shard_map/ppermute | solution.py:641
  96.7 3.5 %collective-permute-start.22 = (bf16[16,1408]{1,0:T(8,128)(2,1)S(1)}, bf16[16,1408]{1,0:T(8,128)(2,1)S(1)}, u32[]{:S(2)}, u32[]{:S(2)}) collective-permute-start(bf16[16,1408]{1,0:T(8,128)(2,1)S(1)} %get-tuple-element.116), channel_id=1, source_target_pairs={{24,0},{8,4},{16,8},{0,12},{28,16},{12,20},{20,24},{4,28},{25,1},{... | collective-permute-start | bytes 135176 | tf_op jit(solution)/shard_map/ppermute | solution.py:641
  101.4 1.4 collective-permute-start.23
  102.8 4.9 %collective-permute-start.24 = (bf16[32,1408]{1,0:T(8,128)(2,1)S(1)}, bf16[32,1408]{1,0:T(8,128)(2,1)S(1)}, u32[]{:S(2)}, u32[]{:S(2)}) collective-permute-start(bf16[32,1408]{1,0:T(8,128)(2,1)S(1)} %add_convert_fusion.2.mine_ref), channel_id=1, source_target_pairs={{0,16},{8,24},{16,0},{24,8},{1,17},{9,25},{17,1},{25,9},{2,18},{10... | collective-permute-start | bytes 270344 | tf_op jit(solution)/shard_map/ppermute | solution.py:649
  108.4 0.9 collective-permute-start.25
  109.3 1.3 collective-permute-start.26
  113.6 5.9 %collective-permute-start.27 = (bf16[16,3072]{1,0:T(8,128)(2,1)S(1)}, bf16[16,3072]{1,0:T(8,128)(2,1)S(1)}, u32[]{:S(2)}, u32[]{:S(2)}) collective-permute-start(bf16[16,3072]{1,0:T(8,128)(2,1)S(1)} %get-tuple-element.121), channel_id=1, source_target_pairs={{0,0},{4,16},{8,8},{12,24},{16,4},{20,20},{24,12},{28,28},{1,1},{5... | collective-permute-start | bytes 294920 | tf_op jit(solution)/shard_map/ppermute | solution.py:636
  114.2 5.2 %collective-permute-start.28 = (bf16[16,3072]{1,0:T(8,128)(2,1)S(1)}, bf16[16,3072]{1,0:T(8,128)(2,1)S(1)}, u32[]{:S(2)}, u32[]{:S(2)}) collective-permute-start(bf16[16,3072]{1,0:T(8,128)(2,1)S(1)} %get-tuple-element.122), channel_id=1, source_target_pairs={{0,8},{4,24},{8,0},{12,16},{16,12},{20,28},{24,4},{28,20},{1,9},{5... | collective-permute-start | bytes 294920 | tf_op jit(solution)/shard_map/ppermute | solution.py:636
  114.5 11.1 %collective-permute-start.29 = (bf16[16,3072]{1,0:T(8,128)(2,1)S(1)}, bf16[16,3072]{1,0:T(8,128)(2,1)S(1)}, u32[]{:S(2)}, u32[]{:S(2)}) collective-permute-start(bf16[16,3072]{1,0:T(8,128)(2,1)S(1)} %get-tuple-element.123), channel_id=1, source_target_pairs={{0,16},{4,0},{8,24},{12,8},{16,20},{20,4},{24,28},{28,12},{1,17},{... | collective-permute-start | bytes 294920 | tf_op jit(solution)/shard_map/ppermute | solution.py:636
  119.2 7.8 %collective-permute-start.30 = (bf16[16,3072]{1,0:T(8,128)(2,1)S(1)}, bf16[16,3072]{1,0:T(8,128)(2,1)S(1)}, u32[]{:S(2)}, u32[]{:S(2)}) collective-permute-start(bf16[16,3072]{1,0:T(8,128)(2,1)S(1)} %get-tuple-element.124), channel_id=1, source_target_pairs={{0,24},{4,8},{8,16},{12,0},{16,28},{20,12},{24,20},{28,4},{1,25},{... | collective-permute-start | bytes 294920 | tf_op jit(solution)/shard_map/ppermute | solution.py:636
  132.3 6.3 %collective-permute-start.31 = (bf16[16,1408]{1,0:T(8,128)(2,1)S(1)}, bf16[16,1408]{1,0:T(8,128)(2,1)S(1)}, u32[]{:S(2)}, u32[]{:S(2)}) collective-permute-start(bf16[16,1408]{1,0:T(8,128)(2,1)S(1)} %get-tuple-element.128), channel_id=1, source_target_pairs={{0,0},{16,4},{8,8},{24,12},{4,16},{20,20},{12,24},{28,28},{1,1},{1... | collective-permute-start | bytes 135176 | tf_op jit(solution)/shard_map/ppermute | solution.py:641
  133.0 5.7 %collective-permute-start.32 = (bf16[16,1408]{1,0:T(8,128)(2,1)S(1)}, bf16[16,1408]{1,0:T(8,128)(2,1)S(1)}, u32[]{:S(2)}, u32[]{:S(2)}) collective-permute-start(bf16[16,1408]{1,0:T(8,128)(2,1)S(1)} %get-tuple-element.129), channel_id=1, source_target_pairs={{8,0},{24,4},{0,8},{16,12},{12,16},{28,20},{4,24},{20,28},{9,1},{2... | collective-permute-start | bytes 135176 | tf_op jit(solution)/shard_map/ppermute | solution.py:641
  133.2 7.7 %collective-permute-start.33 = (bf16[16,1408]{1,0:T(8,128)(2,1)S(1)}, bf16[16,1408]{1,0:T(8,128)(2,1)S(1)}, u32[]{:S(2)}, u32[]{:S(2)}) collective-permute-start(bf16[16,1408]{1,0:T(8,128)(2,1)S(1)} %get-tuple-element.130), channel_id=1, source_target_pairs={{16,0},{0,4},{24,8},{8,12},{20,16},{4,20},{28,24},{12,28},{17,1},{... | collective-permute-start | bytes 135176 | tf_op jit(solution)/shard_map/ppermute | solution.py:641
  138.4 3.5 %collective-permute-start.34 = (bf16[16,1408]{1,0:T(8,128)(2,1)S(1)}, bf16[16,1408]{1,0:T(8,128)(2,1)S(1)}, u32[]{:S(2)}, u32[]{:S(2)}) collective-permute-start(bf16[16,1408]{1,0:T(8,128)(2,1)S(1)} %get-tuple-element.131), channel_id=1, source_target_pairs={{24,0},{8,4},{16,8},{0,12},{28,16},{12,20},{20,24},{4,28},{25,1},{... | collective-permute-start | bytes 135176 | tf_op jit(solution)/shard_map/ppermute | solution.py:641
  143.1 1.4 collective-permute-start.35
  144.5 4.9 %collective-permute-start.36 = (bf16[32,1408]{1,0:T(8,128)(2,1)S(1)}, bf16[32,1408]{1,0:T(8,128)(2,1)S(1)}, u32[]{:S(2)}, u32[]{:S(2)}) collective-permute-start(bf16[32,1408]{1,0:T(8,128)(2,1)S(1)} %add_convert_fusion.1.mine_ref), channel_id=1, source_target_pairs={{0,16},{8,24},{16,0},{24,8},{1,17},{9,25},{17,1},{25,9},{2,18},{10... | collective-permute-start | bytes 270344 | tf_op jit(solution)/shard_map/ppermute | solution.py:649
  150.1 9.5 %collective-permute-start.37 = (bf16[32,1280]{1,0:T(8,128)(2,1)S(1)}, bf16[32,1280]{1,0:T(8,128)(2,1)S(1)}, u32[]{:S(2)}, u32[]{:S(2)}) collective-permute-start(bf16[32,1280]{1,0:T(8,128)(2,1)S(1)} %get-tuple-element.135), channel_id=1, source_target_pairs={{0,1},{1,0},{2,3},{3,2},{4,5},{5,4},{6,7},{7,6},{8,9},{9,8},{10,11... | collective-permute-start | bytes 245768 | tf_op jit(solution)/shard_map/ppermute | solution.py:734
  159.6 1.3 collective-permute-start.38
  163.8 5.8 %collective-permute-start.39 = (bf16[16,3072]{1,0:T(8,128)(2,1)S(1)}, bf16[16,3072]{1,0:T(8,128)(2,1)S(1)}, u32[]{:S(2)}, u32[]{:S(2)}) collective-permute-start(bf16[16,3072]{1,0:T(8,128)(2,1)S(1)} %get-tuple-element.136), channel_id=1, source_target_pairs={{0,0},{4,16},{8,8},{12,24},{16,4},{20,20},{24,12},{28,28},{1,1},{5... | collective-permute-start | bytes 294920 | tf_op jit(solution)/shard_map/ppermute | solution.py:636
  164.5 5.2 %collective-permute-start.40 = (bf16[16,3072]{1,0:T(8,128)(2,1)S(1)}, bf16[16,3072]{1,0:T(8,128)(2,1)S(1)}, u32[]{:S(2)}, u32[]{:S(2)}) collective-permute-start(bf16[16,3072]{1,0:T(8,128)(2,1)S(1)} %get-tuple-element.137), channel_id=1, source_target_pairs={{0,8},{4,24},{8,0},{12,16},{16,12},{20,28},{24,4},{28,20},{1,9},{5... | collective-permute-start | bytes 294920 | tf_op jit(solution)/shard_map/ppermute | solution.py:636
  164.7 11.1 %collective-permute-start.41 = (bf16[16,3072]{1,0:T(8,128)(2,1)S(1)}, bf16[16,3072]{1,0:T(8,128)(2,1)S(1)}, u32[]{:S(2)}, u32[]{:S(2)}) collective-permute-start(bf16[16,3072]{1,0:T(8,128)(2,1)S(1)} %get-tuple-element.138), channel_id=1, source_target_pairs={{0,16},{4,0},{8,24},{12,8},{16,20},{20,4},{24,28},{28,12},{1,17},{... | collective-permute-start | bytes 294920 | tf_op jit(solution)/shard_map/ppermute | solution.py:636
  169.4 7.8 %collective-permute-start.42 = (bf16[16,3072]{1,0:T(8,128)(2,1)S(1)}, bf16[16,3072]{1,0:T(8,128)(2,1)S(1)}, u32[]{:S(2)}, u32[]{:S(2)}) collective-permute-start(bf16[16,3072]{1,0:T(8,128)(2,1)S(1)} %get-tuple-element.139), channel_id=1, source_target_pairs={{0,24},{4,8},{8,16},{12,0},{16,28},{20,12},{24,20},{28,4},{1,25},{... | collective-permute-start | bytes 294920 | tf_op jit(solution)/shard_map/ppermute | solution.py:636
  182.5 13.9 %slice-start = ((s8[5242880]{0:T(1024)(128)(4,1)}), s8[4194304]{0:T(1024)(128)(4,1)S(1)}, s32[]{:S(2)}) async-start(s8[5242880]{0:T(1024)(128)(4,1)} %bitcast.8), calls=%async_computation | async-start | bytes 8388608
  182.5 6.6 %collective-permute-start.43 = (bf16[16,1408]{1,0:T(8,128)(2,1)S(1)}, bf16[16,1408]{1,0:T(8,128)(2,1)S(1)}, u32[]{:S(2)}, u32[]{:S(2)}) collective-permute-start(bf16[16,1408]{1,0:T(8,128)(2,1)S(1)} %get-tuple-element.143), channel_id=1, source_target_pairs={{0,0},{16,4},{8,8},{24,12},{4,16},{20,20},{12,24},{28,28},{1,1},{1... | collective-permute-start | bytes 135176 | tf_op jit(solution)/shard_map/ppermute | solution.py:641
  183.3 5.8 %collective-permute-start.44 = (bf16[16,1408]{1,0:T(8,128)(2,1)S(1)}, bf16[16,1408]{1,0:T(8,128)(2,1)S(1)}, u32[]{:S(2)}, u32[]{:S(2)}) collective-permute-start(bf16[16,1408]{1,0:T(8,128)(2,1)S(1)} %get-tuple-element.144), channel_id=1, source_target_pairs={{8,0},{24,4},{0,8},{16,12},{12,16},{28,20},{4,24},{20,28},{9,1},{2... | collective-permute-start | bytes 135176 | tf_op jit(solution)/shard_map/ppermute | solution.py:641
  183.6 7.8 %collective-permute-start.45 = (bf16[16,1408]{1,0:T(8,128)(2,1)S(1)}, bf16[16,1408]{1,0:T(8,128)(2,1)S(1)}, u32[]{:S(2)}, u32[]{:S(2)}) collective-permute-start(bf16[16,1408]{1,0:T(8,128)(2,1)S(1)} %get-tuple-element.145), channel_id=1, source_target_pairs={{16,0},{0,4},{24,8},{8,12},{20,16},{4,20},{28,24},{12,28},{17,1},{... | collective-permute-start | bytes 135176 | tf_op jit(solution)/shard_map/ppermute | solution.py:641
  188.9 7.6 %slice-start.1 = ((s8[5242880]{0:T(1024)(128)(4,1)}), s8[1048576]{0:T(1024)(128)(4,1)S(1)}, s32[]{:S(2)}) async-start(s8[5242880]{0:T(1024)(128)(4,1)} %bitcast.8), calls=%async_computation.1 | async-start | bytes 2097152
  188.9 3.5 %collective-permute-start.46 = (bf16[16,1408]{1,0:T(8,128)(2,1)S(1)}, bf16[16,1408]{1,0:T(8,128)(2,1)S(1)}, u32[]{:S(2)}, u32[]{:S(2)}) collective-permute-start(bf16[16,1408]{1,0:T(8,128)(2,1)S(1)} %get-tuple-element.146), channel_id=1, source_target_pairs={{24,0},{8,4},{16,8},{0,12},{28,16},{12,20},{20,24},{4,28},{25,1},{... | collective-permute-start | bytes 135176 | tf_op jit(solution)/shard_map/ppermute | solution.py:641
  193.6 1.4 collective-permute-start.47
  195.0 10.1 %collective-permute-start.48 = (bf16[32,1408]{1,0:T(8,128)(2,1)S(1)}, bf16[32,1408]{1,0:T(8,128)(2,1)S(1)}, u32[]{:S(2)}, u32[]{:S(2)}) collective-permute-start(bf16[32,1408]{1,0:T(8,128)(2,1)S(1)} %add_convert_fusion.mine_ref), channel_id=1, source_target_pairs={{0,16},{8,24},{16,0},{24,8},{1,17},{9,25},{17,1},{25,9},{2,18},{10... | collective-permute-start | bytes 270344 | tf_op jit(solution)/shard_map/ppermute | solution.py:649
  196.5 9.9 %copy-start.1 = (f32[1,2560]{1,0:T(1,128)S(1)}, f32[1,2560]{1,0:T(1,128)}, u32[]{:S(2)}) copy-start(f32[1,2560]{1,0:T(1,128)} %param.18) | copy-start | bytes 30724
